TPU v7x, 8 devices: a whole 2x2x1 slice. The times are simulated.
8 devices in a mesh: data: 1 (over z), col: 2 (over y), row: 4 (over x, core).
Axes of the slice: x: 2, y: 2, z: 1, core: 2. Of those that a mesh axis runs over, the one named last changes fastest.
Arguments:
- tokens: bfloat16 [4096, 5120], P(('data', 'row'), 'col')
- w_qkv: bfloat16 [5120, 7168], P('row', 'col')
- w_out: bfloat16 [5120, 5120], P('row', 'col')
- doc_ids: int32 [4096], P(('data', 'row'))
Outputs:
- output: bfloat16 [4096, 5120], P(('data', 'row'), 'col')
All inputs are finite; a program needn't handle non-finite values.
Results may differ from a plain program's by a relative error of at most 0.00408423.
Values are sent between devices in bfloat16 or wider.
A program may use at most 1 GiB of HBM per device.

v0:
```python
import jax
import jax.numpy as jnp
from jax import lax
from jax.sharding import PartitionSpec as P

HEAD_DIM = 128


def block_size(row_count, score_width):
    q_blk = row_count
    while q_blk % 16 == 0 and q_blk * score_width > 4194304:
        q_blk = q_blk // 2
    return q_blk


def solution(mesh):
    score_scale = HEAD_DIM ** -0.5

    def local_block(tokens, w_qkv, w_out, doc_ids):
        rows_loc, cols_loc = tokens.shape
        heads_loc = cols_loc // HEAD_DIM
        groups_loc = (w_qkv.shape[1] - cols_loc) // (2 * HEAD_DIM)
        group_ratio = heads_loc // groups_loc
        x_panel = lax.all_gather(tokens, "col", axis=1, tiled=True)
        w_panel = lax.all_gather(w_qkv, "row", axis=0, tiled=True)
        qkv_rows = jnp.dot(x_panel, w_panel, preferred_element_type=jnp.float32).astype(jnp.bfloat16)
        qkv_rows = qkv_rows.reshape(rows_loc, groups_loc, group_ratio + 2, HEAD_DIM)
        kv_all = lax.all_gather(qkv_rows[:, :, group_ratio:, :], "row", axis=0, tiled=True)
        seg_all = lax.all_gather(doc_ids, "row", axis=0, tiled=True)
        seq_len = kv_all.shape[0]
        key_rows = kv_all[:, :, 0, :]
        value_rows = kv_all[:, :, 1, :]
        q_blk = block_size(rows_loc, heads_loc * seq_len)
        n_steps = rows_loc // q_blk
        q_steps = qkv_rows[:, :, :group_ratio, :].reshape(n_steps, q_blk, groups_loc, group_ratio, HEAD_DIM)

        def attend(block_in):
            q_part, seg_part = block_in
            scores = jnp.einsum("qgrd,kgd->qgrk", q_part, key_rows, preferred_element_type=jnp.float32) * score_scale
            same_doc = seg_part[:, None, None, None] == seg_all[None, None, None, :]
            scores = jnp.where(same_doc, scores, -jnp.inf)
            weights = jax.nn.softmax(scores, axis=-1).astype(jnp.bfloat16)
            context = jnp.einsum("qgrk,kgd->qgrd", weights, value_rows, preferred_element_type=jnp.float32)
            return context.astype(jnp.bfloat16)

        context = lax.map(attend, (q_steps, doc_ids.reshape(n_steps, q_blk)))
        context = context.reshape(rows_loc, cols_loc)
        o_panel = lax.all_gather(context, "col", axis=1, tiled=True)
        wo_panel = lax.all_gather(w_out, "row", axis=0, tiled=True)
        return jnp.dot(o_panel, wo_panel, preferred_element_type=jnp.float32).astype(jnp.bfloat16)

    row_spec = P(("data", "row"), "col")
    weight_spec = P("row", "col")
    return jax.shard_map(local_block, mesh=mesh, in_specs=(row_spec, weight_spec, weight_spec, P(("data", "row"))), out_specs=row_spec, check_vma=False)
```

profile of v0, /device:TPU:0, one launch (start us, length us, event | category | flops | bytes accessed | tf_op | source)
XLA Modules:
  0.0 1259.8 jit_solution(822782274860167047)
XLA Ops:
  8.1 131.2 %all-gather.6.cloned.1.call-done = bf16[1024,5120]{1,0:T(8,128)(2,1)} async-done(((bf16[1024,2560]{1,0:T(8,128)(2,1)}), bf16[1024,5120]{1,0:T(8,128)(2,1)}) %all-gather.6.cloned.1.call-update) | async-done | bytes 10485776 | tf_op jit(solution)/shard_map/all_gather | solution.py:24
  139.2 220.6 %all-gather.8.cloned.1.call-done = bf16[5120,3584]{1,0:T(8,128)(2,1)} async-done(((bf16[1280,3584]{1,0:T(8,128)(2,1)}), bf16[5120,3584]{1,0:T(8,128)(2,1)}) %all-gather.8.cloned.1.call-update) | async-done | bytes 36700176 | tf_op jit(solution)/shard_map/all_gather | solution.py:25
  359.8 45.7 %convolution_convert_fusion = bf16[1024,3584]{1,0:T(8,128)(2,1)} fusion(bf16[1024,5120]{1,0:T(8,128)(2,1)} %all-gather.6.cloned.1.call-done, bf16[5120,3584]{1,0:T(8,128)(2,1)} %all-gather.8.cloned.1.call-done), kind=kOutput, calls=%fused_computation.25 | convolution fusion | flops 37584633856 | bytes 54525952 | tf_op jit(solution)/shard_map/dot_general | solution.py:26
  405.6 10.4 copy.12
  419.8 7.2 all_gather.18
  432.7 7.8 copy.13
  440.5 34.5 %all-gather.10.cloned.1.call-done = bf16[4096,4,2,128]{0,3,2,1:T(8,128)(2,1)} async-done(((bf16[1024,4,2,128]{0,3,2,1:T(8,128)(2,1)}), bf16[4096,4,2,128]{0,3,2,1:T(8,128)(2,1)}) %all-gather.10.cloned.1.call-update) | async-done | bytes 8388624 | tf_op jit(solution)/shard_map/all_gather | solution.py:28
  493.6 576.2 %while.10 = (s32[]{:T(128)}, bf16[32,32,4,5,128]{4,1,3,2,0:T(8,128)(2,1)}, s32[32,32]{1,0:T(8,128)S(1)}, s32[4096]{0:T(1024)S(1)}, bf16[32,32,4,5,128]{4,1,0,3,2...) while((s32[]{:T(128)}, ...), condition=%wide.region_3.4_spmd, body=%wide.region_0.3_spmd.sunk | while | flops 1363365888 | bytes 50944472 | solution.py:46
  497.6 6.6 fusion.44
  504.2 7.4 fusion.45
  515.6 6.6 fusion.44
  522.2 7.4 fusion.45
  533.6 6.6 fusion.44
  540.2 7.4 fusion.45
  551.6 6.6 fusion.44
  558.2 7.4 fusion.45
  576.2 7.4 fusion.45
  594.2 7.4 fusion.45
  612.2 7.4 fusion.45
  630.2 7.4 fusion.45
  648.2 7.4 fusion.45
  666.2 7.4 fusion.45
  684.3 7.4 fusion.45
  702.3 7.4 fusion.45
  720.3 7.4 fusion.45
  738.3 7.4 fusion.45
  756.3 7.4 fusion.45
  774.3 7.4 fusion.45
  792.3 7.4 fusion.45
  810.3 7.4 fusion.45
  828.3 7.4 fusion.45
  846.3 7.4 fusion.45
  864.3 7.4 fusion.45
  882.3 7.4 fusion.45
  900.3 7.4 fusion.45
  918.3 7.4 fusion.45
  936.4 7.4 fusion.45
  954.4 7.4 fusion.45
  972.4 7.4 fusion.45
  990.4 7.4 fusion.45
  1008.4 7.4 fusion.45
  1026.4 7.4 fusion.45
  1044.4 7.4 fusion.45
  1062.4 7.4 fusion.45
  1069.8 8.7 copy.17
  1078.5 12.6 %reshape.49 = bf16[1024,2560]{1,0:T(8,128)(2,1)} reshape(bf16[32,32,4,5,128]{4,3,2,1,0:T(8,128)(2,1)} %copy.17) | data formatting | bytes 10485760 | tf_op jit(solution)/shard_map/reshape | solution.py:47
  1091.2 127.7 %all-gather.12.cloned.1.call-done = bf16[1024,5120]{1,0:T(8,128)(2,1)} async-done(((bf16[1024,2560]{1,0:T(8,128)(2,1)}), bf16[1024,5120]{1,0:T(8,128)(2,1)}) %all-gather.12.cloned.1.call-update) | async-done | bytes 10485776 | tf_op jit(solution)/shard_map/all_gather | solution.py:48
  1218.9 34.4 %convolution_convert_fusion.1 = bf16[1024,2560]{1,0:T(8,128)(2,1)} fusion(bf16[1024,5120]{1,0:T(8,128)(2,1)} %all-gather.12.cloned.1.call-done, bf16[5120,2560]{1,0:T(8,128)(2,1)} %all-gather.14.cloned.1.call-done), kind=kOutput, calls=%fused_computation.26 | convolution fusion | flops 26846167040 | bytes 41943040 | tf_op jit(solution)/shard_map/dot_general | solution.py:50
  (144 shorter events, 341.2 us)
Async XLA Ops:
  6.5 132.7 %all-gather.6.cloned.1.call-start = ((), (), s32[]{:S(2)}) async-start(), calls=%async_computation | async-start | bytes 15728640 | tf_op jit(solution)/shard_map/all_gather | solution.py:24
  7.3 352.6 %all-gather.8.cloned.1.call-start = ((), (), s32[]{:S(2)}) async-start(), calls=%async_computation.1 | async-start | bytes 45875200 | tf_op jit(solution)/shard_map/all_gather | solution.py:25
  8.0 467.0 %all-gather.10.cloned.1.call-start = ((), (), s32[]{:S(2)}) async-start(), calls=%async_computation.2 | async-start | bytes 10485760 | tf_op jit(solution)/shard_map/all_gather | solution.py:28
  416.0 3.7 copy-start
  419.1 672.1 %all-gather.14.cloned.1.call-start = ((), (), s32[]{:S(2)}) async-start(), calls=%async_computation.4 | async-start | bytes 32768000 | tf_op jit(solution)/shard_map/all_gather | solution.py:49
  419.7 799.2 %all-gather.12.cloned.1.call-start = ((), (), s32[]{:S(2)}) async-start(), calls=%async_computation.3 | async-start | bytes 15728640 | tf_op jit(solution)/shard_map/all_gather | solution.py:48
Sparse Core Ops, SparseCore 0:
  8.9 130.3 all-gather.5
  140.8 219.0 all-gather.7
  419.2 55.7 all-gather.9
  476.4 158.6 all-gather.13
  1091.3 127.5 all-gather.11
where the time goes:
time: 1260 us
  waiting for transfers between devices  516 us (41%)
  matrix products  440 us (35%)
  other arithmetic  216 us (17%)
  local copies, waits for them, and re-layouts  67.4 us (5%)
  between operations  13.2 us (1%)
    dot_general x32, matrix products, attend(): jnp.einsum('qgrk,kgd->qgrd', weights, value_rows, preferred_element_type=...  238 us
    all_gather x1, waiting for transfers between devices, local_block(): w_panel = lax.all_gather(w_qkv, 'row', axis=0, tiled=True)  221 us
    sub x32, other arithmetic, attend(): weights = jax.nn.softmax(scores, axis=-1).astype(jnp.bfloat16)  211 us
    all_gather x1, waiting for transfers between devices, local_block(): x_panel = lax.all_gather(tokens, 'col', axis=1, tiled=True)  131 us
    all_gather x1, waiting for transfers between devices, local_block(): o_panel = lax.all_gather(context, 'col', axis=1, tiled=True)  128 us
    dot_general x32, matrix products, attend(): jnp.einsum('qgrd,kgd->qgrk', q_part, key_rows, preferred_element_type=jnp...  122 us
    dot_general x1, matrix products, local_block(): jnp.dot(x_panel, w_panel, preferred_element_type=jnp.float32)  45.7 us
    all_gather x1, waiting for transfers between devices, local_block(): lax.all_gather(qkv_rows[:, :, group_ratio:, :], 'row', axis=0, tiled=True)  34.5 us
  transfers between devices with their start and end apart: 5, of which 4 were waited for; matrix products, arithmetic and copies ran while one was open for 50% of the time, Pallas kernels for 0%

commit v1 on v0

v1 whole, which is shorter than its diff:
```python
import functools

import jax
import jax.numpy as jnp
from jax import lax
from jax.experimental import pallas as pl
from jax.experimental.pallas import tpu as pltpu
from jax.sharding import PartitionSpec as P


HEAD_DIM = 128
LOG2E = 1.4426950408889634
VMEM_LIMIT = 60 * 1024 * 1024
OUT_CHUNKS = 4
Q_TILE = 512


def n_tiles(width):
    return [(lo, min(256, width - lo)) for lo in range(0, width, 256)]


def project_kernel(n_own, piece, offset, width, splits, refs):
    xs, (w_own, w_near, w_far, w_last) = refs[:2 * n_own], refs[2 * n_own:2 * n_own + 4]
    outs = refs[-5 - len(splits):-5]
    panel, weights, total, x_sems, w_sems = refs[-5:]
    row, col = lax.axis_index("row"), lax.axis_index("col")
    x_width = 2 * piece // n_own
    parts = max(piece // x_width, 1)
    copies = []
    for i, ref in enumerate(xs):
        side = col if i < n_own else 1 - col
        start = (i % n_own) * x_width
        for lo in range(0, x_width, min(x_width, piece)):
            at = start + lo
            slot = row ^ (side * 2 + at // piece)
            size = min(x_width, piece)
            copies.append(pltpu.make_async_copy(
                ref.at[:, pl.ds(lo, size)], panel.at[slot, :, pl.ds(at % piece, size)],
                x_sems.at[slot, (at % piece) // size]))
    columns = pl.ds(offset, width)
    w_copies = [
        pltpu.make_async_copy(w_own.at[:, columns], weights.at[0], w_sems.at[0]),
        pltpu.make_async_copy(w_near.at[:, columns], weights.at[1], w_sems.at[1]),
        pltpu.make_async_copy(w_far, weights.at[2], w_sems.at[2]),
        pltpu.make_async_copy(w_last, weights.at[3], w_sems.at[3]),
    ]
    w_copies[0].start()
    for copy in copies:
        copy.start()
    for copy in w_copies[1:]:
        copy.start()
    size = min(x_width, piece)
    for j in range(4):
        w_copies[j].wait()
        for k in range(parts):
            at = panel.at[j, :, pl.ds(k * size, size)]
            pltpu.make_async_copy(at, at, x_sems.at[j, k]).wait()
        for lo, n in n_tiles(width):
            here = pl.ds(lo, n)
            term = jnp.dot(panel[j], weights[j, :, here], preferred_element_type=jnp.float32)
            if j > 0:
                term += total[:, here]
            if j < 3:
                total[:, here] = term
            else:
                for out, first, last in zip(outs, (0,) + splits[:-1], splits):
                    a, b = max(lo, first), min(lo + n, last)
                    if a < b:
                        out[:, a - first:b - first] = term[:, a - lo:b - lo].astype(out.dtype)


def project(own, other, w_own, w_near, w_far, w_last, offset, splits):
    rows = own[0].shape[0]
    piece, width = w_far.shape
    n_own = len(own)
    ends = (0,) + splits[:-1]

    def body(*refs):
        project_kernel(n_own, piece, offset, width, splits, refs)

    return pl.pallas_call(
        body,
        out_shape=[jax.ShapeDtypeStruct((rows, b - a), jnp.bfloat16) for a, b in zip(ends, splits)],
        in_specs=[pl.BlockSpec(memory_space=pl.ANY)] * (2 * n_own + 4),
        out_specs=[pl.BlockSpec(memory_space=pltpu.VMEM)] * len(splits),
        scratch_shapes=[
            pltpu.VMEM((4, rows, piece), jnp.bfloat16),
            pltpu.VMEM((4, piece, width), jnp.bfloat16),
            pltpu.VMEM((rows, width), jnp.float32),
            pltpu.SemaphoreType.DMA((4, 2)),
            pltpu.SemaphoreType.DMA((4,)),
        ],
        compiler_params=pltpu.CompilerParams(vmem_limit_bytes=VMEM_LIMIT),
        cost_estimate=pl.CostEstimate(flops=2 * rows * 4 * piece * width, bytes_accessed=8 * piece * (rows + width), transcendentals=0),
    )(*own, *other, w_own, w_near, w_far, w_last)


def attention_kernel(n, bq, docs, q_ref, k0, k1, k2, k3, q_doc, k_doc, out_ref, kv, sems, p0, p1, l0, l1, acc, big):
    i = pl.program_id(0)
    row = lax.axis_index("row")
    bk = k0.shape[0]
    d = HEAD_DIM

    @pl.when(i == 0)
    def _():
        copies = [pltpu.make_async_copy(ref, kv.at[row ^ j], sems.at[j]) for j, ref in enumerate((k0, k1, k2, k3))]
        for copy in copies:
            copy.start()
        for copy in copies:
            copy.wait()

    def ends(kb):
        at = (row ^ kb) * bk
        return docs[at], docs[at + bk - 1]

    q_lo, q_hi = docs[i * bq], docs[i * bq + bq - 1]
    lo, hi = jnp.int32(0), jnp.int32(0)
    for kb in range(4):
        k_lo, k_hi = ends(kb)
        lo += (k_hi < q_lo).astype(jnp.int32)
        hi += (k_lo <= q_hi).astype(jnp.int32)

    scale = d ** -0.5 * LOG2E
    probs, sums = (p0, p1), (l0, l1)

    def cols_of(u):
        return pl.ds(pl.multiple_of(u * d, d), d)

    def fold(x, op):
        y = x[:, :d]
        for t in range(1, bk // d):
            y = op(y, x[:, t * d:(t + 1) * d])
        return y

    def scores(u, kb, masked):
        s = lax.dot_general(q_ref[:, cols_of(u)], kv[kb, :, :d], (((1,), (1,)), ((), ())), preferred_element_type=jnp.float32)
        if masked:
            s = jnp.where(q_doc[...] == k_doc[row ^ kb], s, -jnp.inf)
        return s

    def stage(first, second, phase, exact=False):
        p_a, l_a = probs[phase % 2], sums[phase % 2]
        p_c, l_c = probs[(phase - 1) % 2], sums[(phase - 1) % 2]
        if first is not None:
            if exact:
                acc[...] = jnp.full(acc.shape, -jnp.inf, jnp.float32)

                @pl.loop(lo, hi)
                def _(kb):
                    acc[...] = jnp.maximum(acc[...], fold(scores(first, kb, True), jnp.maximum))

                top = jnp.max(acc[...], axis=1, keepdims=True)
            else:
                own = kv[row, pl.ds(pl.multiple_of(i * bq, bq), bq), :d].astype(jnp.float32)
                top = jnp.sum(q_ref[:, cols_of(first)].astype(jnp.float32) * own, axis=1, keepdims=True)
            l_a[...] = jnp.zeros_like(l_a)
        if second is not None:
            total = jnp.sum(l_c[...], axis=1, keepdims=True)
            if not exact:
                big[...] = jnp.maximum(big[...], total)
            inv = 1.0 / total
            acc[...] = jnp.zeros_like(acc)

        def step(kb, masked):
            if second is not None:
                p = (p_c[kb] * inv).astype(jnp.bfloat16)
                acc[...] += jnp.dot(p, kv[kb, :, d:], preferred_element_type=jnp.float32)
            if first is not None:
                p = jnp.exp2((scores(first, kb, masked) - top) * scale)
                p_a[kb] = p
                l_a[...] += fold(p, jnp.add)

        @pl.loop(lo, hi)
        def _(kb):
            if first is None or exact:
                step(kb, exact)
            else:
                k_lo, k_hi = ends(kb)
                plain = (q_lo == q_hi) & (q_lo == k_lo) & (q_lo == k_hi)

                @pl.when(plain)
                def _():
                    step(kb, False)

                @pl.when(jnp.logical_not(plain))
                def _():
                    step(kb, True)

        if second is not None:
            out_ref[:, cols_of(second)] = acc[...].astype(out_ref.dtype)

    big[...] = jnp.zeros_like(big)
    stage(0, None, 0)

    @pl.loop(0, (n - 1) // 2)
    def _(k):
        stage(2 * k + 1, 2 * k, 1)
        stage(2 * k + 2, 2 * k + 1, 2)

    for u in range(1 + 2 * ((n - 1) // 2), n):
        stage(u, u - 1, u)
    stage(None, n - 1, n)

    @pl.when(jnp.logical_not(jnp.max(big[...]) < 1e30))
    def _():
        @pl.loop(0, n)
        def _(u):
            stage(u, None, 0, True)
            stage(None, u, 1, True)


def attention(queries, kv_pieces, docs, q_doc, k_doc):
    rows, width = queries.shape
    n = width // HEAD_DIM
    bk = kv_pieces[0].shape[0]
    bq = min(Q_TILE, rows)
    grid_spec = pltpu.PrefetchScalarGridSpec(
        num_scalar_prefetch=1,
        grid=(rows // bq,),
        in_specs=[pl.BlockSpec((bq, width), lambda i, _: (i, 0))]
        + [pl.BlockSpec(memory_space=pl.ANY)] * 4
        + [pl.BlockSpec((bq, 1), lambda i, _: (i, 0)), pl.BlockSpec(k_doc.shape, lambda i, _: (0, 0, 0))],
        out_specs=pl.BlockSpec((bq, width), lambda i, _: (i, 0)),
        scratch_shapes=[pltpu.VMEM((4, bk, 2 * HEAD_DIM), jnp.bfloat16), pltpu.SemaphoreType.DMA((4,))]
        + [pltpu.VMEM((4, bq, bk), jnp.float32)] * 2
        + [pltpu.VMEM((bq, HEAD_DIM), jnp.float32)] * 3
        + [pltpu.VMEM((bq, 1), jnp.float32)],
    )
    return pl.pallas_call(
        functools.partial(attention_kernel, n, bq),
        grid_spec=grid_spec,
        out_shape=jax.ShapeDtypeStruct((rows, width), jnp.bfloat16),
        compiler_params=pltpu.CompilerParams(vmem_limit_bytes=VMEM_LIMIT),
        cost_estimate=pl.CostEstimate(flops=16 * rows * 4 * bk * width, bytes_accessed=4 * rows * width, transcendentals=rows * 4 * bk * n),
    )(docs, queries, *kv_pieces, q_doc, k_doc)


def solution(mesh):
    n_row = mesh.shape["row"]
    over_x = [(r, r ^ 2) for r in range(n_row)]
    over_core = [(r, r ^ 1) for r in range(n_row)]
    over_y = [(0, 1), (1, 0)]

    def far(piece):
        return lax.ppermute(piece, "row", over_x)

    def near(piece):
        return lax.ppermute(piece, "row", over_core)

    def after(value, *others):
        return lax.optimization_barrier((value,) + others)[0]

    def local_block(tokens, w_qkv, w_out, doc_ids):
        rows, cols = tokens.shape
        groups = (w_qkv.shape[1] - cols) // (2 * HEAD_DIM)
        q_cols = cols // groups
        g_cols = q_cols + 2 * HEAD_DIM
        n_cols = cols // OUT_CHUNKS

        tokens_y = lax.ppermute(tokens, "col", over_y)
        docs_x = far(doc_ids)
        w_far = [far(w_qkv[:, g * g_cols:(g + 1) * g_cols]) for g in range(3)]
        w_near = near(w_qkv)
        docs = jnp.concatenate([doc_ids, near(doc_ids), docs_x, near(docs_x)])
        q_doc, k_doc = doc_ids.reshape(rows, 1), docs.reshape(n_row, 1, rows)
        wo_near = near(w_out)
        wo_far = []

        def project_group(g, x_y):
            w_last = near(w_far[g])
            q, kv = project([tokens], [x_y], w_qkv, w_near, w_far[g], w_last, g * g_cols, (q_cols, g_cols))
            kv_x = far(kv)
            return q, [kv, near(kv), kv_x, near(kv_x)]

        own, other = [], []

        def attend(q, pieces):
            context = attention(q, pieces, docs, q_doc, k_doc)
            own.append(context)
            other.append(lax.ppermute(context, "col", over_y))

        q0, kv0 = project_group(0, tokens_y)
        q1, kv1 = project_group(1, after(tokens_y, kv0[0]))
        q2, kv2 = project_group(2, after(tokens_y, kv1[0]))
        w_far.append(far(after(w_qkv[:, 3 * g_cols:], kv2[0])))
        wo_far.append(far(after(w_out[:, :n_cols], kv2[0])))
        attend(after(q0, q2), kv0)
        attend(after(q1, own[0]), kv1)
        q3, kv3 = project_group(3, after(tokens_y, own[1]))
        for c in range(1, OUT_CHUNKS):
            wo_far.append(far(after(w_out[:, c * n_cols:(c + 1) * n_cols], kv3[0])))
        attend(after(q2, kv3[0]), kv2)
        attend(after(q3, own[2]), kv3)
        parts = [
            project(own, other, w_out, wo_near, wo_far[c], near(wo_far[c]), c * n_cols, (n_cols,))[0]
            for c in range(OUT_CHUNKS)
        ]
        return jnp.concatenate(parts, axis=1)

    row_spec = P(("data", "row"), "col")
    weight_spec = P("row", "col")
    return jax.shard_map(local_block, mesh=mesh, in_specs=(row_spec, weight_spec, weight_spec, P(("data", "row"))), out_specs=row_spec, check_vma=False)
```

time: 1260 us -> 605 us (0.48)
  the two profiles are of different devices: /device:TPU:0 before, /device:TPU:5 now
where the time goes in v1:
time: 605 us; the launch traced here: 595 us
  Pallas kernels  316 us (52%)
  waiting for transfers between devices  237 us (39%)
  starting transfers between devices  21.8 us (4%)
  local copies, waits for them, and re-layouts  15.8 us (3%)
    ppermute x13, waiting for transfers between devices, far(): return lax.ppermute(piece, 'row', over_x)  235 us
    pallas_call x4, Pallas kernels, attention(): pl.pallas_call(functools.partial(attention_kernel, n, bq), grid_spec=grid...  161 us
    pallas_call x8, Pallas kernels, project(): pl.pallas_call(body, out_shape=[jax.ShapeDtypeStruct((rows, b - a), jnp.b...  154 us
  transfers between devices with their start and end apart: 38, of which 8 were waited for; matrix products, arithmetic and copies ran while one was open for 2% of the time, Pallas kernels for 50%

profile of v1, /device:TPU:5, one launch (start us, length us, event | category | flops | bytes accessed | tf_op | source)
XLA Modules:
  0.0 595.4 jit_solution(16417946509810229202)
XLA Ops:
  0.0 0.7 collective-permute-start.4
  0.7 5.1 fusion
  5.8 1.4 collective-permute-start.5
  7.3 1.4 collective-permute-start.1
  8.7 97.8 %collective-permute-done.1 = s32[1024]{0:T(1024)S(1)} collective-permute-done((s32[1024]{0:T(1024)S(1)}, s32[1024]{0:T(1024)S(1)}, u32[]{:S(2)}, u32[]{:S(2)}) %collective-permute-start.1) | collective-permute-done | bytes 4128 | tf_op jit(solution)/shard_map/ppermute | solution.py:245
  106.5 0.9 collective-permute-start
  107.4 0.8 collective-permute-done
  108.2 0.3 collective-permute-start.2
  108.6 0.8 collective-permute-done.2
  109.4 1.4 collective-permute-start.9
  110.8 0.6 collective-permute-start.6
  111.5 1.1 copy.5.q_doc
  112.5 48.2 %collective-permute-done.9.refs_4_ = bf16[1280,896]{1,0:T(8,128)(2,1)} collective-permute-done((bf16[1280,896]{1,0:T(8,128)(2,1)}, bf16[1280,896]{1,0:T(8,128)(2,1)}, u32[]{:S(2)}, u32[]{:S(2)}) %collective-permute-start.9) | collective-permute-done | bytes 2293792 | tf_op jit(solution)/shard_map/ppermute | solution.py:245
  160.8 1.2 collective-permute-start.10
  162.0 0.6 pad_add_fusion.k_doc
  162.6 18.9 %shard_map.46 = (bf16[1024,640]{1,0:T(8,128)(2,1)}, bf16[1024,256]{1,0:T(8,128)(2,1)}) custom-call(bf16[1024,2560]{1,0:T(8,128)(2,1)} %refs_0_.7, bf16[1024,2560]{1,0:T(8,128)(2,1)} %collective-permute-done.3.refs_1_, bf16[1280,3584]{1,0:T(8,128)(2,1)} %refs_2_.7, bf16[1280,3584]{1,0:T(8,128)(2,1)} %collective-permute-done.4.refs_3_, ...), custom_call_target="tpu_custom_call" | custom-call | flops 9395240960 | bytes 19660800 | tf_op jit(solution)/shard_map/pallas_call | solution.py:81
  181.6 18.9 %shard_map.47 = (bf16[1024,640]{1,0:T(8,128)(2,1)}, bf16[1024,256]{1,0:T(8,128)(2,1)}) custom-call(bf16[1024,2560]{1,0:T(8,128)(2,1)} %refs_0_.7, bf16[1024,2560]{1,0:T(8,128)(2,1)} %collective-permute-done.3.refs_1_, bf16[1280,3584]{1,0:T(8,128)(2,1)} %refs_2_.7, bf16[1280,3584]{1,0:T(8,128)(2,1)} %collective-permute-done.4.refs_3_, ...), custom_call_target="tpu_custom_call" | custom-call | flops 9395240960 | bytes 19660800 | tf_op jit(solution)/shard_map/pallas_call | solution.py:81
  200.6 0.5 collective-permute-start.13
  201.1 19.1 %shard_map.48 = (bf16[1024,640]{1,0:T(8,128)(2,1)}, bf16[1024,256]{1,0:T(8,128)(2,1)}) custom-call(bf16[1024,2560]{1,0:T(8,128)(2,1)} %refs_0_.7, bf16[1024,2560]{1,0:T(8,128)(2,1)} %collective-permute-done.3.refs_1_, bf16[1280,3584]{1,0:T(8,128)(2,1)} %refs_2_.7, bf16[1280,3584]{1,0:T(8,128)(2,1)} %collective-permute-done.4.refs_3_, ...), custom_call_target="tpu_custom_call" | custom-call | flops 9395240960 | bytes 19660800 | tf_op jit(solution)/shard_map/pallas_call | solution.py:81
  220.3 1.4 collective-permute-start.17
  221.8 40.1 %shard_map.49.refs_0_ = bf16[1024,640]{1,0:T(8,128)(2,1)} custom-call(s32[4096]{0:T(1024)} %copy-done.9, bf16[1024,640]{1,0:T(8,128)(2,1)} %get-tuple-element.31.q_ref, bf16[1024,256]{1,0:T(8,128)(2,1)} %get-tuple-element.26.k0, bf16[1024,256]{1,0:T(8,128)(2,1)} %collective-permute-done.11.k1, bf16[1024,256]{1,0:T(8,128)(2,1)} %copy-done.13, ...), custom_call_target="tpu_custom_call" | custom-call | flops 42949672960 | bytes 2621440 | tf_op jit(solution)/shard_map/pallas_call | solution.py:229
  261.9 0.5 collective-permute-start.21
  262.4 21.1 %collective-permute-done.17.refs_4_ = bf16[1280,896]{1,0:T(8,128)(2,1)} collective-permute-done((bf16[1280,896]{1,0:T(8,128)(2,1)S(1)}, bf16[1280,896]{1,0:T(8,128)(2,1)}, u32[]{:S(2)}, u32[]{:S(2)}) %collective-permute-start.17) | collective-permute-done | bytes 2293792 | tf_op jit(solution)/shard_map/ppermute | solution.py:245
  283.5 0.4 collective-permute-start.18
  283.9 40.4 %shard_map.50.refs_1_ = bf16[1024,640]{1,0:T(8,128)(2,1)} custom-call(s32[4096]{0:T(1024)} %copy-done.9, bf16[1024,640]{1,0:T(8,128)(2,1)} %get-tuple-element.33.q_ref, bf16[1024,256]{1,0:T(8,128)(2,1)} %get-tuple-element.28.k0, bf16[1024,256]{1,0:T(8,128)(2,1)} %copy-done.12, bf16[1024,256]{1,0:T(8,128)(2,1)} %copy-done.11, ...), custom_call_target="tpu_custom_call" | custom-call | flops 42949672960 | bytes 2621440 | tf_op jit(solution)/shard_map/pallas_call | solution.py:229
  324.4 1.4 copy-done.10
  325.8 18.9 %shard_map.51 = (bf16[1024,640]{1,0:T(8,128)(2,1)}, bf16[1024,256]{1,0:T(8,128)(2,1)}) custom-call(bf16[1024,2560]{1,0:T(8,128)(2,1)} %refs_0_.7, bf16[1024,2560]{1,0:T(8,128)(2,1)} %collective-permute-done.3.refs_1_, bf16[1280,3584]{1,0:T(8,128)(2,1)} %refs_2_.7, bf16[1280,3584]{1,0:T(8,128)(2,1)} %collective-permute-done.4.refs_3_, ...), custom_call_target="tpu_custom_call" | custom-call | flops 9395240960 | bytes 19660800 | tf_op jit(solution)/shard_map/pallas_call | solution.py:81
  344.7 6.0 %fusion.1 = (bf16[1280,640]{1,0:T(8,128)(2,1)}, bf16[1280,640]{1,0:T(8,128)(2,1)}, bf16[1280,640]{1,0:T(8,128)(2,1)}, bf16[1280,640]{1,0:T(8,128)(2,1)}) fusion(bf16[1280,2560]{1,0:T(8,128)(2,1)} %refs_8_.7), kind=kLoop, calls=%fused_computation.7 | loop fusion | bytes 13107200 | tf_op jit(solution)/shard_map/slice | solution.py:286
  350.7 1.4 collective-permute-start.30
  352.1 1.3 collective-permute-start.26
  353.4 5.4 collective-permute-done.23.k2
  358.7 40.5 %shard_map.52.refs_2_ = bf16[1024,640]{1,0:T(8,128)(2,1)} custom-call(s32[4096]{0:T(1024)} %copy-done.9, bf16[1024,640]{1,0:T(8,128)(2,1)} %get-tuple-element.38.q_ref, bf16[1024,256]{1,0:T(8,128)(2,1)} %get-tuple-element.35.k0, bf16[1024,256]{1,0:T(8,128)(2,1)} %collective-permute-done.19.k1, bf16[1024,256]{1,0:T(8,128)(2,1)} %collective-permute-done.20.k2, ...), custom_call_target="tpu_custom_call" | custom-call | flops 42949672960 | bytes 2621440 | tf_op jit(solution)/shard_map/pallas_call | solution.py:229
  399.3 1.4 collective-permute-start.25
  400.7 2.2 collective-permute-start.32
  403.0 1.4 collective-permute-start.36
  404.4 40.4 %shard_map.53.refs_3_ = bf16[1024,640]{1,0:T(8,128)(2,1)} custom-call(s32[4096]{0:T(1024)} %copy-done.9, bf16[1024,640]{1,0:T(8,128)(2,1)} %get-tuple-element.40.q_ref, bf16[1024,256]{1,0:T(8,128)(2,1)} %get-tuple-element.37.k0, bf16[1024,256]{1,0:T(8,128)(2,1)} %collective-permute-done.22.k1, bf16[1024,256]{1,0:T(8,128)(2,1)} %collective-permute-done.23.k2, ...), custom_call_target="tpu_custom_call" | custom-call | flops 42949672960 | bytes 2621440 | tf_op jit(solution)/shard_map/pallas_call | solution.py:229
  444.9 1.4 collective-permute-start.28
  446.3 28.2 %collective-permute-done.34.refs_10_ = bf16[1280,640]{1,0:T(8,128)(2,1)} collective-permute-done((bf16[1280,640]{1,0:T(8,128)(2,1)}, bf16[1280,640]{1,0:T(8,128)(2,1)}, u32[]{:S(2)}, u32[]{:S(2)}) %collective-permute-start.34) | collective-permute-done | bytes 1638432 | tf_op jit(solution)/shard_map/ppermute | solution.py:245
  474.5 0.8 collective-permute-start.35
  475.4 34.3 %collective-permute-done.36.refs_10_ = bf16[1280,640]{1,0:T(8,128)(2,1)} collective-permute-done((bf16[1280,640]{1,0:T(8,128)(2,1)}, bf16[1280,640]{1,0:T(8,128)(2,1)}, u32[]{:S(2)}, u32[]{:S(2)}) %collective-permute-start.36) | collective-permute-done | bytes 1638432 | tf_op jit(solution)/shard_map/ppermute | solution.py:245
  509.6 0.6 collective-permute-start.37
  510.3 1.1 copy-done.3
  511.3 1.1 copy-done.4
  512.4 19.4 %shard_map.54 = bf16[1024,640]{1,0:T(8,128)(2,1)} custom-call(bf16[1024,640]{1,0:T(8,128)(2,1)} %shard_map.49.refs_0_, bf16[1024,640]{1,0:T(8,128)(2,1)} %shard_map.50.refs_1_, bf16[1024,640]{1,0:T(8,128)(2,1)} %shard_map.52.refs_2_, bf16[1024,640]{1,0:T(8,128)(2,1)} %shard_map.53.refs_3_, bf16[1024,640]{1,0:T(8,128)(2,1)} %collective-permute-done.25.refs_4_, ...), custom_call_target="tpu_custom_call" | custom-call | flops 6710886400 | bytes 17039360 | tf_op jit(solution)/shard_map/pallas_call | solution.py:81
  531.8 19.7 %shard_map.55 = bf16[1024,640]{1,0:T(8,128)(2,1)} custom-call(bf16[1024,640]{1,0:T(8,128)(2,1)} %shard_map.49.refs_0_, bf16[1024,640]{1,0:T(8,128)(2,1)} %shard_map.50.refs_1_, bf16[1024,640]{1,0:T(8,128)(2,1)} %shard_map.52.refs_2_, bf16[1024,640]{1,0:T(8,128)(2,1)} %shard_map.53.refs_3_, bf16[1024,640]{1,0:T(8,128)(2,1)} %collective-permute-done.25.refs_4_, ...), custom_call_target="tpu_custom_call" | custom-call | flops 6710886400 | bytes 17039360 | tf_op jit(solution)/shard_map/pallas_call | solution.py:81
  551.5 19.5 %shard_map.56 = bf16[1024,640]{1,0:T(8,128)(2,1)} custom-call(bf16[1024,640]{1,0:T(8,128)(2,1)} %shard_map.49.refs_0_, bf16[1024,640]{1,0:T(8,128)(2,1)} %shard_map.50.refs_1_, bf16[1024,640]{1,0:T(8,128)(2,1)} %shard_map.52.refs_2_, bf16[1024,640]{1,0:T(8,128)(2,1)} %shard_map.53.refs_3_, bf16[1024,640]{1,0:T(8,128)(2,1)} %collective-permute-done.25.refs_4_, ...), custom_call_target="tpu_custom_call" | custom-call | flops 6710886400 | bytes 17039360 | tf_op jit(solution)/shard_map/pallas_call | solution.py:81
  571.1 19.9 %shard_map.57 = bf16[1024,640]{1,0:T(8,128)(2,1)} custom-call(bf16[1024,640]{1,0:T(8,128)(2,1)} %shard_map.49.refs_0_, bf16[1024,640]{1,0:T(8,128)(2,1)} %shard_map.50.refs_1_, bf16[1024,640]{1,0:T(8,128)(2,1)} %shard_map.52.refs_2_, bf16[1024,640]{1,0:T(8,128)(2,1)} %shard_map.53.refs_3_, bf16[1024,640]{1,0:T(8,128)(2,1)} %collective-permute-done.25.refs_4_, ...), custom_call_target="tpu_custom_call" | custom-call | flops 6710886400 | bytes 17039360 | tf_op jit(solution)/shard_map/pallas_call | solution.py:81
  591.0 3.9 pad_maximum_fusion
  (77 shorter events, 0.5 us)
Async XLA Ops:
  0.0 162.6 %collective-permute-start.4 = (bf16[1280,3584]{1,0:T(8,128)(2,1)}, bf16[1280,3584]{1,0:T(8,128)(2,1)}, u32[]{:S(2)}, u32[]{:S(2)}) collective-permute-start(bf16[1280,3584]{1,0:T(8,128)(2,1)} %refs_2_.7), channel_id=1, source_target_pairs={{0,1},{1,0},{2,3},{3,2},{4,5},{5,4},{6,7},{7,6}} | collective-permute-start | bytes 27525128 | tf_op jit(solution)/shard_map/ppermute | solution.py:248
  0.7 161.9 %collective-permute-start.3 = (bf16[1024,2560]{1,0:T(8,128)(2,1)}, bf16[1024,2560]{1,0:T(8,128)(2,1)}, u32[]{:S(2)}, u32[]{:S(2)}) collective-permute-start(bf16[1024,2560]{1,0:T(8,128)(2,1)} %refs_0_.7), channel_id=1, source_target_pairs={{0,4},{4,0},{1,5},{5,1},{2,6},{6,2},{3,7},{7,3}} | collective-permute-start | bytes 15728648 | tf_op jit(solution)/shard_map/ppermute | solution.py:260
  5.8 105.0 %collective-permute-start.5 = (bf16[1280,896]{1,0:T(8,128)(2,1)S(1)}, bf16[1280,896]{1,0:T(8,128)(2,1)}, u32[]{:S(2)}, u32[]{:S(2)}) collective-permute-start(bf16[1280,896]{1,0:T(8,128)(2,1)S(1)} %get-tuple-element.48), channel_id=1, source_target_pairs={{0,2},{1,3},{2,0},{3,1},{4,6},{5,7},{6,4},{7,5}} | collective-permute-start | bytes 6881288 | tf_op jit(solution)/shard_map/ppermute | solution.py:245
  7.3 104.2 %collective-permute-start.7 = (bf16[1280,896]{1,0:T(8,128)(2,1)S(1)}, bf16[1280,896]{1,0:T(8,128)(2,1)}, u32[]{:S(2)}, u32[]{:S(2)}) collective-permute-start(bf16[1280,896]{1,0:T(8,128)(2,1)S(1)} %get-tuple-element.47), channel_id=1, source_target_pairs={{0,2},{1,3},{2,0},{3,1},{4,6},{5,7},{6,4},{7,5}} | collective-permute-start | bytes 6881288 | tf_op jit(solution)/shard_map/ppermute | solution.py:245
  7.3 99.2 %collective-permute-start.1 = (s32[1024]{0:T(1024)S(1)}, s32[1024]{0:T(1024)S(1)}, u32[]{:S(2)}, u32[]{:S(2)}) collective-permute-start(s32[1024]{0:T(1024)S(1)} %copy-done.8), channel_id=1, source_target_pairs={{0,2},{1,3},{2,0},{3,1},{4,6},{5,7},{6,4},{7,5}} | collective-permute-start | bytes 12296 | tf_op jit(solution)/shard_map/ppermute | solution.py:245
  106.5 1.7 collective-permute-start
  108.2 1.2 collective-permute-start.2
  109.4 51.4 %collective-permute-start.9 = (bf16[1280,896]{1,0:T(8,128)(2,1)}, bf16[1280,896]{1,0:T(8,128)(2,1)}, u32[]{:S(2)}, u32[]{:S(2)}) collective-permute-start(bf16[1280,896]{1,0:T(8,128)(2,1)} %get-tuple-element.46), channel_id=1, source_target_pairs={{0,2},{1,3},{2,0},{3,1},{4,6},{5,7},{6,4},{7,5}} | collective-permute-start | bytes 6881288 | tf_op jit(solution)/shard_map/ppermute | solution.py:245
  110.8 51.8 %collective-permute-start.6 = (bf16[1280,896]{1,0:T(8,128)(2,1)}, bf16[1280,896]{1,0:T(8,128)(2,1)}, u32[]{:S(2)}, u32[]{:S(2)}) collective-permute-start(bf16[1280,896]{1,0:T(8,128)(2,1)} %collective-permute-done.5.refs_4_), channel_id=1, source_target_pairs={{0,1},{1,0},{2,3},{3,2},{4,5},{5,4},{6,7},{7,6}} | collective-permute-start | bytes 6881288 | tf_op jit(solution)/shard_map/ppermute | solution.py:248
  111.4 70.1 %collective-permute-start.8 = (bf16[1280,896]{1,0:T(8,128)(2,1)}, bf16[1280,896]{1,0:T(8,128)(2,1)}, u32[]{:S(2)}, u32[]{:S(2)}) collective-permute-start(bf16[1280,896]{1,0:T(8,128)(2,1)} %collective-permute-done.7.refs_4_), channel_id=1, source_target_pairs={{0,1},{1,0},{2,3},{3,2},{4,5},{5,4},{6,7},{7,6}} | collective-permute-start | bytes 6881288 | tf_op jit(solution)/shard_map/ppermute | solution.py:248
  160.8 39.8 %collective-permute-start.10 = (bf16[1280,896]{1,0:T(8,128)(2,1)}, bf16[1280,896]{1,0:T(8,128)(2,1)}, u32[]{:S(2)}, u32[]{:S(2)}) collective-permute-start(bf16[1280,896]{1,0:T(8,128)(2,1)} %collective-permute-done.9.refs_4_), channel_id=1, source_target_pairs={{0,1},{1,0},{2,3},{3,2},{4,5},{5,4},{6,7},{7,6}} | collective-permute-start | bytes 6881288 | tf_op jit(solution)/shard_map/ppermute | solution.py:248
  162.0 19.5 %copy-start.9 = (s32[4096]{0:T(1024)}, s32[4096]{0:T(1024)S(1)}, u32[]{:S(2)}) copy-start(s32[4096]{0:T(1024)S(1)} %constant_dynamic-update-slice_fusion.docs) | copy-start | bytes 49156
  162.6 236.7 %collective-permute-start.29 = (bf16[1280,2560]{1,0:T(8,128)(2,1)}, bf16[1280,2560]{1,0:T(8,128)(2,1)}, u32[]{:S(2)}, u32[]{:S(2)}) collective-permute-start(bf16[1280,2560]{1,0:T(8,128)(2,1)} %refs_8_.7), channel_id=1, source_target_pairs={{0,1},{1,0},{2,3},{3,2},{4,5},{5,4},{6,7},{7,6}} | collective-permute-start | bytes 19660808 | tf_op jit(solution)/shard_map/ppermute | solution.py:248
  181.5 19.1 %collective-permute-start.12 = (bf16[1024,256]{1,0:T(8,128)(2,1)}, bf16[1024,256]{1,0:T(8,128)(2,1)S(1)}, u32[]{:S(2)}, u32[]{:S(2)}) collective-permute-start(bf16[1024,256]{1,0:T(8,128)(2,1)} %get-tuple-element.26.k0), channel_id=1, source_target_pairs={{0,2},{1,3},{2,0},{3,1},{4,6},{5,7},{6,4},{7,5}} | collective-permute-start | bytes 1572872 | tf_op jit(solution)/shard_map/ppermute | solution.py:245
  181.6 38.7 %collective-permute-start.11 = (bf16[1024,256]{1,0:T(8,128)(2,1)}, bf16[1024,256]{1,0:T(8,128)(2,1)}, u32[]{:S(2)}, u32[]{:S(2)}) collective-permute-start(bf16[1024,256]{1,0:T(8,128)(2,1)} %get-tuple-element.26.k0), channel_id=1, source_target_pairs={{0,1},{1,0},{2,3},{3,2},{4,5},{5,4},{6,7},{7,6}} | collective-permute-start | bytes 1572872 | tf_op jit(solution)/shard_map/ppermute | solution.py:248
  200.5 19.8 %collective-permute-start.15 = (bf16[1024,256]{1,0:T(8,128)(2,1)}, bf16[1024,256]{1,0:T(8,128)(2,1)S(1)}, u32[]{:S(2)}, u32[]{:S(2)}) collective-permute-start(bf16[1024,256]{1,0:T(8,128)(2,1)} %get-tuple-element.28.k0), channel_id=1, source_target_pairs={{0,2},{1,3},{2,0},{3,1},{4,6},{5,7},{6,4},{7,5}} | collective-permute-start | bytes 1572872 | tf_op jit(solution)/shard_map/ppermute | solution.py:245
  200.6 61.3 %collective-permute-start.14 = (bf16[1024,256]{1,0:T(8,128)(2,1)}, bf16[1024,256]{1,0:T(8,128)(2,1)S(1)}, u32[]{:S(2)}, u32[]{:S(2)}) collective-permute-start(bf16[1024,256]{1,0:T(8,128)(2,1)} %get-tuple-element.28.k0), channel_id=1, source_target_pairs={{0,1},{1,0},{2,3},{3,2},{4,5},{5,4},{6,7},{7,6}} | collective-permute-start | bytes 1572872 | tf_op jit(solution)/shard_map/ppermute | solution.py:248
  200.6 19.6 %copy-start.13 = (bf16[1024,256]{1,0:T(8,128)(2,1)}, bf16[1024,256]{1,0:T(8,128)(2,1)S(1)}, u32[]{:S(2)}) copy-start(bf16[1024,256]{1,0:T(8,128)(2,1)S(1)} %collective-permute-done.12.k2) | copy-start | bytes 1572868
  200.6 21.1 %collective-permute-start.13 = (bf16[1024,256]{1,0:T(8,128)(2,1)S(1)}, bf16[1024,256]{1,0:T(8,128)(2,1)}, u32[]{:S(2)}, u32[]{:S(2)}) collective-permute-start(bf16[1024,256]{1,0:T(8,128)(2,1)S(1)} %collective-permute-done.12.k2), channel_id=1, source_target_pairs={{0,1},{1,0},{2,3},{3,2},{4,5},{5,4},{6,7},{7,6}} | collective-permute-start | bytes 1572872 | tf_op jit(solution)/shard_map/ppermute | solution.py:248
  220.2 41.7 %collective-permute-start.20 = (bf16[1024,256]{1,0:T(8,128)(2,1)}, bf16[1024,256]{1,0:T(8,128)(2,1)}, u32[]{:S(2)}, u32[]{:S(2)}) collective-permute-start(bf16[1024,256]{1,0:T(8,128)(2,1)} %get-tuple-element.35.k0), channel_id=1, source_target_pairs={{0,2},{1,3},{2,0},{3,1},{4,6},{5,7},{6,4},{7,5}} | collective-permute-start | bytes 1572872 | tf_op jit(solution)/shard_map/ppermute | solution.py:245
  220.3 41.5 %copy-start.11 = (bf16[1024,256]{1,0:T(8,128)(2,1)}, bf16[1024,256]{1,0:T(8,128)(2,1)S(1)}, u32[]{:S(2)}) copy-start(bf16[1024,256]{1,0:T(8,128)(2,1)S(1)} %collective-permute-done.15.k2) | copy-start | bytes 1572868
  220.3 63.2 %collective-permute-start.17 = (bf16[1280,896]{1,0:T(8,128)(2,1)S(1)}, bf16[1280,896]{1,0:T(8,128)(2,1)}, u32[]{:S(2)}, u32[]{:S(2)}) collective-permute-start(bf16[1280,896]{1,0:T(8,128)(2,1)S(1)} %get-tuple-element.36), channel_id=1, source_target_pairs={{0,2},{1,3},{2,0},{3,1},{4,6},{5,7},{6,4},{7,5}} | collective-permute-start | bytes 6881288 | tf_op jit(solution)/shard_map/ppermute | solution.py:245
  221.7 62.2 %collective-permute-start.16 = (bf16[1024,256]{1,0:T(8,128)(2,1)S(1)}, bf16[1024,256]{1,0:T(8,128)(2,1)}, u32[]{:S(2)}, u32[]{:S(2)}) collective-permute-start(bf16[1024,256]{1,0:T(8,128)(2,1)S(1)} %collective-permute-done.15.k2), channel_id=1, source_target_pairs={{0,1},{1,0},{2,3},{3,2},{4,5},{5,4},{6,7},{7,6}} | collective-permute-start | bytes 1572872 | tf_op jit(solution)/shard_map/ppermute | solution.py:248
  261.9 22.1 %copy-start.12 = (bf16[1024,256]{1,0:T(8,128)(2,1)}, bf16[1024,256]{1,0:T(8,128)(2,1)S(1)}, u32[]{:S(2)}) copy-start(bf16[1024,256]{1,0:T(8,128)(2,1)S(1)} %collective-permute-done.14.k1) | copy-start | bytes 1572868
  261.9 90.2 %collective-permute-start.19 = (bf16[1024,256]{1,0:T(8,128)(2,1)}, bf16[1024,256]{1,0:T(8,128)(2,1)}, u32[]{:S(2)}, u32[]{:S(2)}) collective-permute-start(bf16[1024,256]{1,0:T(8,128)(2,1)} %get-tuple-element.35.k0), channel_id=1, source_target_pairs={{0,1},{1,0},{2,3},{3,2},{4,5},{5,4},{6,7},{7,6}} | collective-permute-start | bytes 1572872 | tf_op jit(solution)/shard_map/ppermute | solution.py:248
  261.9 91.5 %collective-permute-start.21 = (bf16[1024,256]{1,0:T(8,128)(2,1)}, bf16[1024,256]{1,0:T(8,128)(2,1)}, u32[]{:S(2)}, u32[]{:S(2)}) collective-permute-start(bf16[1024,256]{1,0:T(8,128)(2,1)} %collective-permute-done.20.k2), channel_id=1, source_target_pairs={{0,1},{1,0},{2,3},{3,2},{4,5},{5,4},{6,7},{7,6}} | collective-permute-start | bytes 1572872 | tf_op jit(solution)/shard_map/ppermute | solution.py:248
  283.5 40.9 %collective-permute-start.18 = (bf16[1280,896]{1,0:T(8,128)(2,1)}, bf16[1280,896]{1,0:T(8,128)(2,1)S(1)}, u32[]{:S(2)}, u32[]{:S(2)}) collective-permute-start(bf16[1280,896]{1,0:T(8,128)(2,1)} %collective-permute-done.17.refs_4_), channel_id=1, source_target_pairs={{0,1},{1,0},{2,3},{3,2},{4,5},{5,4},{6,7},{7,6}} | collective-permute-start | bytes 6881288 | tf_op jit(solution)/shard_map/ppermute | solution.py:248
  344.7 7.4 %copy-start.1 = (bf16[1024,640]{1,0:T(8,128)(2,1)S(1)}, bf16[1024,640]{1,0:T(8,128)(2,1)}, u32[]{:S(2)}) copy-start(bf16[1024,640]{1,0:T(8,128)(2,1)} %shard_map.50.refs_1_) | copy-start | bytes 3932164
  344.7 14.1 %collective-permute-start.23 = (bf16[1024,256]{1,0:T(8,128)(2,1)}, bf16[1024,256]{1,0:T(8,128)(2,1)}, u32[]{:S(2)}, u32[]{:S(2)}) collective-permute-start(bf16[1024,256]{1,0:T(8,128)(2,1)} %get-tuple-element.37.k0), channel_id=1, source_target_pairs={{0,2},{1,3},{2,0},{3,1},{4,6},{5,7},{6,4},{7,5}} | collective-permute-start | bytes 1572872 | tf_op jit(solution)/shard_map/ppermute | solution.py:245
  350.7 48.6 %copy-start = (bf16[1024,640]{1,0:T(8,128)(2,1)S(1)}, bf16[1024,640]{1,0:T(8,128)(2,1)}, u32[]{:S(2)}) copy-start(bf16[1024,640]{1,0:T(8,128)(2,1)} %shard_map.49.refs_0_) | copy-start | bytes 3932164
  350.7 50.0 %collective-permute-start.30 = (bf16[1280,640]{1,0:T(8,128)(2,1)}, bf16[1280,640]{1,0:T(8,128)(2,1)}, u32[]{:S(2)}, u32[]{:S(2)}) collective-permute-start(bf16[1280,640]{1,0:T(8,128)(2,1)} %get-tuple-element.41), channel_id=1, source_target_pairs={{0,2},{1,3},{2,0},{3,1},{4,6},{5,7},{6,4},{7,5}} | collective-permute-start | bytes 4915208 | tf_op jit(solution)/shard_map/ppermute | solution.py:245
  352.1 48.6 %collective-permute-start.26 = (bf16[1024,640]{1,0:T(8,128)(2,1)S(1)}, bf16[1024,640]{1,0:T(8,128)(2,1)S(1)}, u32[]{:S(2)}, u32[]{:S(2)}) collective-permute-start(bf16[1024,640]{1,0:T(8,128)(2,1)S(1)} %copy-done.1), channel_id=1, source_target_pairs={{0,4},{4,0},{1,5},{5,1},{2,6},{6,2},{3,7},{7,3}} | collective-permute-start | bytes 3932168 | tf_op jit(solution)/shard_map/ppermute | solution.py:280
  353.4 49.6 %collective-permute-start.22 = (bf16[1024,256]{1,0:T(8,128)(2,1)}, bf16[1024,256]{1,0:T(8,128)(2,1)}, u32[]{:S(2)}, u32[]{:S(2)}) collective-permute-start(bf16[1024,256]{1,0:T(8,128)(2,1)} %get-tuple-element.37.k0), channel_id=1, source_target_pairs={{0,1},{1,0},{2,3},{3,2},{4,5},{5,4},{6,7},{7,6}} | collective-permute-start | bytes 1572872 | tf_op jit(solution)/shard_map/ppermute | solution.py:248
  358.7 44.3 %collective-permute-start.24 = (bf16[1024,256]{1,0:T(8,128)(2,1)}, bf16[1024,256]{1,0:T(8,128)(2,1)}, u32[]{:S(2)}, u32[]{:S(2)}) collective-permute-start(bf16[1024,256]{1,0:T(8,128)(2,1)} %collective-permute-done.23.k2), channel_id=1, source_target_pairs={{0,1},{1,0},{2,3},{3,2},{4,5},{5,4},{6,7},{7,6}} | collective-permute-start | bytes 1572872 | tf_op jit(solution)/shard_map/ppermute | solution.py:248
  399.3 45.5 %collective-permute-start.25 = (bf16[1024,640]{1,0:T(8,128)(2,1)S(1)}, bf16[1024,640]{1,0:T(8,128)(2,1)}, u32[]{:S(2)}, u32[]{:S(2)}) collective-permute-start(bf16[1024,640]{1,0:T(8,128)(2,1)S(1)} %copy-done), channel_id=1, source_target_pairs={{0,4},{4,0},{1,5},{5,1},{2,6},{6,2},{3,7},{7,3}} | collective-permute-start | bytes 3932168 | tf_op jit(solution)/shard_map/ppermute | solution.py:280
  400.7 44.2 %collective-permute-start.31 = (bf16[1280,640]{1,0:T(8,128)(2,1)}, bf16[1280,640]{1,0:T(8,128)(2,1)}, u32[]{:S(2)}, u32[]{:S(2)}) collective-permute-start(bf16[1280,640]{1,0:T(8,128)(2,1)} %collective-permute-done.30.refs_10_), channel_id=1, source_target_pairs={{0,1},{1,0},{2,3},{3,2},{4,5},{5,4},{6,7},{7,6}} | collective-permute-start | bytes 4915208 | tf_op jit(solution)/shard_map/ppermute | solution.py:248
  400.7 44.1 %copy-start.2 = (bf16[1024,640]{1,0:T(8,128)(2,1)}, bf16[1024,640]{1,0:T(8,128)(2,1)S(1)}, u32[]{:S(2)}) copy-start(bf16[1024,640]{1,0:T(8,128)(2,1)S(1)} %collective-permute-done.26.refs_5_) | copy-start | bytes 3932164
  400.7 45.6 %collective-permute-start.32 = (bf16[1280,640]{1,0:T(8,128)(2,1)}, bf16[1280,640]{1,0:T(8,128)(2,1)}, u32[]{:S(2)}, u32[]{:S(2)}) collective-permute-start(bf16[1280,640]{1,0:T(8,128)(2,1)} %get-tuple-element.42), channel_id=1, source_target_pairs={{0,2},{1,3},{2,0},{3,1},{4,6},{5,7},{6,4},{7,5}} | collective-permute-start | bytes 4915208 | tf_op jit(solution)/shard_map/ppermute | solution.py:245
  403.0 71.6 %collective-permute-start.34 = (bf16[1280,640]{1,0:T(8,128)(2,1)}, bf16[1280,640]{1,0:T(8,128)(2,1)}, u32[]{:S(2)}, u32[]{:S(2)}) collective-permute-start(bf16[1280,640]{1,0:T(8,128)(2,1)} %get-tuple-element.43), channel_id=1, source_target_pairs={{0,2},{1,3},{2,0},{3,1},{4,6},{5,7},{6,4},{7,5}} | collective-permute-start | bytes 4915208 | tf_op jit(solution)/shard_map/ppermute | solution.py:245
  403.0 106.6 %collective-permute-start.36 = (bf16[1280,640]{1,0:T(8,128)(2,1)}, bf16[1280,640]{1,0:T(8,128)(2,1)}, u32[]{:S(2)}, u32[]{:S(2)}) collective-permute-start(bf16[1280,640]{1,0:T(8,128)(2,1)} %get-tuple-element.44), channel_id=1, source_target_pairs={{0,2},{1,3},{2,0},{3,1},{4,6},{5,7},{6,4},{7,5}} | collective-permute-start | bytes 4915208 | tf_op jit(solution)/shard_map/ppermute | solution.py:245
  444.8 65.4 %collective-permute-start.27 = (bf16[1024,640]{1,0:T(8,128)(2,1)}, bf16[1024,640]{1,0:T(8,128)(2,1)S(1)}, u32[]{:S(2)}, u32[]{:S(2)}) collective-permute-start(bf16[1024,640]{1,0:T(8,128)(2,1)} %shard_map.52.refs_2_), channel_id=1, source_target_pairs={{0,4},{4,0},{1,5},{5,1},{2,6},{6,2},{3,7},{7,3}} | collective-permute-start | bytes 3932168 | tf_op jit(solution)/shard_map/ppermute | solution.py:280
  444.9 65.4 %collective-permute-start.28 = (bf16[1024,640]{1,0:T(8,128)(2,1)}, bf16[1024,640]{1,0:T(8,128)(2,1)S(1)}, u32[]{:S(2)}, u32[]{:S(2)}) collective-permute-start(bf16[1024,640]{1,0:T(8,128)(2,1)} %shard_map.53.refs_3_), channel_id=1, source_target_pairs={{0,4},{4,0},{1,5},{5,1},{2,6},{6,2},{3,7},{7,3}} | collective-permute-start | bytes 3932168 | tf_op jit(solution)/shard_map/ppermute | solution.py:280
  446.3 85.5 %collective-permute-start.33 = (bf16[1280,640]{1,0:T(8,128)(2,1)}, bf16[1280,640]{1,0:T(8,128)(2,1)}, u32[]{:S(2)}, u32[]{:S(2)}) collective-permute-start(bf16[1280,640]{1,0:T(8,128)(2,1)} %collective-permute-done.32.refs_10_), channel_id=1, source_target_pairs={{0,1},{1,0},{2,3},{3,2},{4,5},{5,4},{6,7},{7,6}} | collective-permute-start | bytes 4915208 | tf_op jit(solution)/shard_map/ppermute | solution.py:248
  474.5 77.0 %collective-permute-start.35 = (bf16[1280,640]{1,0:T(8,128)(2,1)}, bf16[1280,640]{1,0:T(8,128)(2,1)}, u32[]{:S(2)}, u32[]{:S(2)}) collective-permute-start(bf16[1280,640]{1,0:T(8,128)(2,1)} %collective-permute-done.34.refs_10_), channel_id=1, source_target_pairs={{0,1},{1,0},{2,3},{3,2},{4,5},{5,4},{6,7},{7,6}} | collective-permute-start | bytes 4915208 | tf_op jit(solution)/shard_map/ppermute | solution.py:248
  509.6 61.5 %collective-permute-start.37 = (bf16[1280,640]{1,0:T(8,128)(2,1)}, bf16[1280,640]{1,0:T(8,128)(2,1)}, u32[]{:S(2)}, u32[]{:S(2)}) collective-permute-start(bf16[1280,640]{1,0:T(8,128)(2,1)} %collective-permute-done.36.refs_10_), channel_id=1, source_target_pairs={{0,1},{1,0},{2,3},{3,2},{4,5},{5,4},{6,7},{7,6}} | collective-permute-start | bytes 4915208 | tf_op jit(solution)/shard_map/ppermute | solution.py:248
  571.1 19.9 %copy-start.5 = (bf16[1024,640]{1,0:T(8,128)(2,1)S(1)}, bf16[1024,640]{1,0:T(8,128)(2,1)}, u32[]{:S(2)}) copy-start(bf16[1024,640]{1,0:T(8,128)(2,1)} %shard_map.54) | copy-start | bytes 3932164
  571.1 19.9 %copy-start.6 = (bf16[1024,640]{1,0:T(8,128)(2,1)S(1)}, bf16[1024,640]{1,0:T(8,128)(2,1)}, u32[]{:S(2)}) copy-start(bf16[1024,640]{1,0:T(8,128)(2,1)} %shard_map.55) | copy-start | bytes 3932164
  571.1 19.9 %copy-start.7 = (bf16[1024,640]{1,0:T(8,128)(2,1)S(1)}, bf16[1024,640]{1,0:T(8,128)(2,1)}, u32[]{:S(2)}) copy-start(bf16[1024,640]{1,0:T(8,128)(2,1)} %shard_map.56) | copy-start | bytes 3932164
  (4 other events, 10.9 us)

commit v2 on v1

--- a/solution.py
+++ b/solution.py
@@ -11,7 +11,7 @@
 HEAD_DIM = 128
 LOG2E = 1.4426950408889634
 VMEM_LIMIT = 60 * 1024 * 1024
-OUT_CHUNKS = 4
+OUT_CHUNKS = (512, 1280, 768)
 Q_TILE = 512
 
 
@@ -95,25 +95,76 @@
     )(*own, *other, w_own, w_near, w_far, w_last)
 
 
-def attention_kernel(n, bq, docs, q_ref, k0, k1, k2, k3, q_doc, k_doc, out_ref, kv, sems, p0, p1, l0, l1, acc, big):
-    i = pl.program_id(0)
+def combine_kernel(spots, piece, refs):
+    n_x = len(spots)
+    xs, ws, out = refs[:n_x], refs[n_x:n_x + 4], refs[-3]
+    panel, sems = refs[-2:]
+    row, col = lax.axis_index("row"), lax.axis_index("col")
+
+    def copy_of(i):
+        is_own, at, top = spots[i]
+        side = col if is_own else 1 - col
+        height, width = xs[i].shape
+        return pltpu.make_async_copy(
+            xs[i], panel.at[row ^ (side * 2 + at // piece), pl.ds(top, height), pl.ds(at % piece, width)], sems.at[i])
+
+    @pl.when(pl.program_id(0) == 0)
+    def _():
+        for i in range(n_x):
+            copy_of(i).start()
+        for i in range(n_x):
+            copy_of(i).wait()
+
+    total = jnp.dot(panel[0], ws[0][...], preferred_element_type=jnp.float32)
+    for j in range(1, 4):
+        total += jnp.dot(panel[j], ws[j][...], preferred_element_type=jnp.float32)
+    out[...] = total.astype(out.dtype)
+
+
+def combine(xs, spots, rows, w_own, w_near, w_far, w_last, first, base):
+    piece, width = w_far.shape
+    tile = 256
+    skip = first // tile
+    whole = pl.BlockSpec((piece, tile), lambda n: (0, n + skip))
+    chunk = pl.BlockSpec((piece, tile), lambda n: (0, n))
+    extra = [] if base is None else [base]
+
+    def body(*refs):
+        kept = refs[:len(xs) + 4] + refs[len(xs) + 4 + len(extra):]
+        combine_kernel(spots, piece, kept)
+
+    return pl.pallas_call(
+        body,
+        grid=(width // tile,),
+        out_shape=jax.ShapeDtypeStruct((rows, w_own.shape[1]), jnp.bfloat16),
+        in_specs=[pl.BlockSpec(memory_space=pl.ANY)] * len(xs) + [whole, whole, chunk, chunk]
+        + [pl.BlockSpec(memory_space=pl.ANY)] * len(extra),
+        out_specs=pl.BlockSpec((rows, tile), lambda n: (0, n + skip)),
+        scratch_shapes=[pltpu.VMEM((4, rows, piece), jnp.bfloat16), pltpu.SemaphoreType.DMA((len(xs),))],
+        input_output_aliases={len(xs) + 4: 0} if extra else {},
+        compiler_params=pltpu.CompilerParams(vmem_limit_bytes=VMEM_LIMIT),
+        cost_estimate=pl.CostEstimate(flops=2 * rows * 4 * piece * width, bytes_accessed=8 * piece * (rows + width), transcendentals=0),
+    )(*xs, w_own, w_near, w_far, w_last, *extra)
+
+
+def attention_kernel(heads, bq, start, docs, q_ref, k0, k1, k2, k3, q_doc, k_doc, out_ref, kv, sems, p0, p1, l0, l1, acc, big):
+    rows = q_ref.shape[0]
+    n = heads * (rows // bq)
     row = lax.axis_index("row")
     bk = k0.shape[0]
     d = HEAD_DIM
 
-    @pl.when(i == 0)
-    def _():
-        copies = [pltpu.make_async_copy(ref, kv.at[row ^ j], sems.at[j]) for j, ref in enumerate((k0, k1, k2, k3))]
-        for copy in copies:
-            copy.start()
-        for copy in copies:
-            copy.wait()
+    copies = [pltpu.make_async_copy(ref, kv.at[row ^ j], sems.at[j]) for j, ref in enumerate((k0, k1, k2, k3))]
+    for copy in copies:
+        copy.start()
+    for copy in copies:
+        copy.wait()
 
     def ends(kb):
         at = (row ^ kb) * bk
         return docs[at], docs[at + bk - 1]
 
-    q_lo, q_hi = docs[i * bq], docs[i * bq + bq - 1]
+    q_lo, q_hi = docs[start], docs[start + rows - 1]
     lo, hi = jnp.int32(0), jnp.int32(0)
     for kb in range(4):
         k_lo, k_hi = ends(kb)
@@ -124,7 +175,10 @@
     probs, sums = (p0, p1), (l0, l1)
 
     def cols_of(u):
-        return pl.ds(pl.multiple_of(u * d, d), d)
+        return pl.ds(pl.multiple_of(u % heads * d, d), d)
+
+    def rows_of(u):
+        return pl.ds(pl.multiple_of(u // heads * bq, bq), bq)
 
     def fold(x, op):
         y = x[:, :d]
@@ -133,9 +187,9 @@
         return y
 
     def scores(u, kb, masked):
-        s = lax.dot_general(q_ref[:, cols_of(u)], kv[kb, :, :d], (((1,), (1,)), ((), ())), preferred_element_type=jnp.float32)
+        s = lax.dot_general(q_ref[rows_of(u), cols_of(u)], kv[kb, :, :d], (((1,), (1,)), ((), ())), preferred_element_type=jnp.float32)
         if masked:
-            s = jnp.where(q_doc[...] == k_doc[row ^ kb], s, -jnp.inf)
+            s = jnp.where(q_doc[rows_of(u), :] == k_doc[row ^ kb], s, -jnp.inf)
         return s
 
     def stage(first, second, phase, exact=False):
@@ -151,8 +205,8 @@
 
                 top = jnp.max(acc[...], axis=1, keepdims=True)
             else:
-                own = kv[row, pl.ds(pl.multiple_of(i * bq, bq), bq), :d].astype(jnp.float32)
-                top = jnp.sum(q_ref[:, cols_of(first)].astype(jnp.float32) * own, axis=1, keepdims=True)
+                own = kv[row, pl.ds(pl.multiple_of(start + first // heads * bq, bq), bq), :d].astype(jnp.float32)
+                top = jnp.sum(q_ref[rows_of(first), cols_of(first)].astype(jnp.float32) * own, axis=1, keepdims=True)
             l_a[...] = jnp.zeros_like(l_a)
         if second is not None:
             total = jnp.sum(l_c[...], axis=1, keepdims=True)
@@ -187,7 +241,7 @@
                     step(kb, True)
 
         if second is not None:
-            out_ref[:, cols_of(second)] = acc[...].astype(out_ref.dtype)
+            out_ref[rows_of(second), cols_of(second)] = acc[...].astype(out_ref.dtype)
 
     big[...] = jnp.zeros_like(big)
     stage(0, None, 0)
@@ -209,29 +263,30 @@
             stage(None, u, 1, True)
 
 
-def attention(queries, kv_pieces, docs, q_doc, k_doc):
-    rows, width = queries.shape
-    n = width // HEAD_DIM
+def attention(queries, kv_pieces, docs, q_doc, k_doc, start, rows):
+    width = queries.shape[1]
+    heads = width // HEAD_DIM
     bk = kv_pieces[0].shape[0]
     bq = min(Q_TILE, rows)
+    here = start // rows
     grid_spec = pltpu.PrefetchScalarGridSpec(
         num_scalar_prefetch=1,
-        grid=(rows // bq,),
-        in_specs=[pl.BlockSpec((bq, width), lambda i, _: (i, 0))]
+        grid=(1,),
+        in_specs=[pl.BlockSpec((rows, width), lambda i, _: (here, 0))]
         + [pl.BlockSpec(memory_space=pl.ANY)] * 4
-        + [pl.BlockSpec((bq, 1), lambda i, _: (i, 0)), pl.BlockSpec(k_doc.shape, lambda i, _: (0, 0, 0))],
-        out_specs=pl.BlockSpec((bq, width), lambda i, _: (i, 0)),
+        + [pl.BlockSpec((rows, 1), lambda i, _: (here, 0)), pl.BlockSpec(k_doc.shape, lambda i, _: (0, 0, 0))],
+        out_specs=pl.BlockSpec((rows, width), lambda i, _: (0, 0)),
         scratch_shapes=[pltpu.VMEM((4, bk, 2 * HEAD_DIM), jnp.bfloat16), pltpu.SemaphoreType.DMA((4,))]
         + [pltpu.VMEM((4, bq, bk), jnp.float32)] * 2
         + [pltpu.VMEM((bq, HEAD_DIM), jnp.float32)] * 3
         + [pltpu.VMEM((bq, 1), jnp.float32)],
     )
     return pl.pallas_call(
-        functools.partial(attention_kernel, n, bq),
+        functools.partial(attention_kernel, heads, bq, start),
         grid_spec=grid_spec,
         out_shape=jax.ShapeDtypeStruct((rows, width), jnp.bfloat16),
         compiler_params=pltpu.CompilerParams(vmem_limit_bytes=VMEM_LIMIT),
-        cost_estimate=pl.CostEstimate(flops=16 * rows * 4 * bk * width, bytes_accessed=4 * rows * width, transcendentals=rows * 4 * bk * n),
+        cost_estimate=pl.CostEstimate(flops=16 * rows * 4 * bk * width, bytes_accessed=4 * rows * width, transcendentals=rows * 4 * bk * heads),
     )(docs, queries, *kv_pieces, q_doc, k_doc)
 
 
@@ -255,16 +310,19 @@
         groups = (w_qkv.shape[1] - cols) // (2 * HEAD_DIM)
         q_cols = cols // groups
         g_cols = q_cols + 2 * HEAD_DIM
-        n_cols = cols // OUT_CHUNKS
+        out_at = [sum(OUT_CHUNKS[:c]) for c in range(len(OUT_CHUNKS))]
+        out_ends = [lo + n for lo, n in zip(out_at, OUT_CHUNKS)]
 
         tokens_y = lax.ppermute(tokens, "col", over_y)
         docs_x = far(doc_ids)
-        w_far = [far(w_qkv[:, g * g_cols:(g + 1) * g_cols]) for g in range(3)]
+        w_slice = w_qkv[:, :g_cols]
+        w_far = [far(w_slice)]
+        w_rest = after(w_qkv, w_slice)
+        w_far += [far(w_rest[:, g * g_cols:(g + 1) * g_cols]) for g in range(1, groups)]
         w_near = near(w_qkv)
         docs = jnp.concatenate([doc_ids, near(doc_ids), docs_x, near(docs_x)])
         q_doc, k_doc = doc_ids.reshape(rows, 1), docs.reshape(n_row, 1, rows)
         wo_near = near(w_out)
-        wo_far = []
 
         def project_group(g, x_y):
             w_last = near(w_far[g])
@@ -272,30 +330,31 @@
             kv_x = far(kv)
             return q, [kv, near(kv), kv_x, near(kv_x)]
 
-        own, other = [], []
-
-        def attend(q, pieces):
-            context = attention(q, pieces, docs, q_doc, k_doc)
-            own.append(context)
-            other.append(lax.ppermute(context, "col", over_y))
+        parts, spots = [], []
+
+        def attend(g, q, pieces, start, size):
+            context = attention(q, pieces, docs, q_doc, k_doc, start, size)
+            context_y = lax.ppermute(context, "col", over_y)
+            parts.extend([context, context_y])
+            spots.extend([(True, g * q_cols, start), (False, g * q_cols, start)])
+            return context
 
         q0, kv0 = project_group(0, tokens_y)
         q1, kv1 = project_group(1, after(tokens_y, kv0[0]))
         q2, kv2 = project_group(2, after(tokens_y, kv1[0]))
-        w_far.append(far(after(w_qkv[:, 3 * g_cols:], kv2[0])))
-        wo_far.append(far(after(w_out[:, :n_cols], kv2[0])))
-        attend(after(q0, q2), kv0)
-        attend(after(q1, own[0]), kv1)
-        q3, kv3 = project_group(3, after(tokens_y, own[1]))
-        for c in range(1, OUT_CHUNKS):
-            wo_far.append(far(after(w_out[:, c * n_cols:(c + 1) * n_cols], kv3[0])))
-        attend(after(q2, kv3[0]), kv2)
-        attend(after(q3, own[2]), kv3)
-        parts = [
-            project(own, other, w_out, wo_near, wo_far[c], near(wo_far[c]), c * n_cols, (n_cols,))[0]
-            for c in range(OUT_CHUNKS)
-        ]
-        return jnp.concatenate(parts, axis=1)
+        out0 = attend(0, after(q0, q2), kv0, 0, rows)
+        q3, kv3 = project_group(3, after(tokens_y, out0))
+        out1 = attend(1, after(q1, q3), kv1, 0, rows)
+        out2 = attend(2, after(q2, out1), kv2, 0, rows)
+        out3 = attend(3, after(q3, out2), kv3, 0, rows // 2)
+        attend(3, after(q3, out3), kv3, rows // 2, rows // 2)
+        wo_rest = after(w_out, kv1[0])
+        wo_far = [far(wo_rest[:, lo:hi]) for lo, hi in zip(out_at, out_ends)]
+        result = None
+        for c, first in enumerate(out_at):
+            w_last = near(wo_far[c])
+            result = combine(parts, spots, rows, w_out, wo_near, wo_far[c], w_last, first, result)
+        return result
 
     row_spec = P(("data", "row"), "col")
     weight_spec = P("row", "col")

time: 605 us -> 629 us (1.040)
  the two profiles are of different devices: /device:TPU:5 before, /device:TPU:2 now
where the time goes in v2:
time: 629 us; the launch traced here: 619 us
  Pallas kernels  288 us (46%)
  waiting for transfers between devices  282 us (45%)
  starting transfers between devices  28.6 us (5%)
  local copies, waits for them, and re-layouts  19.4 us (3%)
    ppermute x12, waiting for transfers between devices, far(): return lax.ppermute(piece, 'row', over_x)  232 us
    pallas_call x5, Pallas kernels, attention(): pl.pallas_call(functools.partial(attention_kernel, heads, bq, start), gri...  165 us
    pallas_call x4, Pallas kernels, project(): pl.pallas_call(body, out_shape=[jax.ShapeDtypeStruct((rows, b - a), jnp.b...  73.6 us
    pallas_call x3, Pallas kernels, combine(): pl.pallas_call(body, grid=(width // tile,), out_shape=jax.ShapeDtypeStruc...  49.3 us
    ppermute x5, waiting for transfers between devices, attend(): context_y = lax.ppermute(context, 'col', over_y)  47.1 us
    ppermute x12, starting transfers between devices, far(): return lax.ppermute(piece, 'row', over_x)  18.4 us
  transfers between devices with their start and end apart: 37, of which 10 were waited for; matrix products, arithmetic and copies ran while one was open for 3% of the time, Pallas kernels for 44%

profile of v2, /device:TPU:2, one launch (start us, length us, event | category | flops | bytes accessed | tf_op | source)
XLA Modules:
  0.0 619.2 jit_solution(334695775002185545)
XLA Ops:
  0.0 1.5 collective-permute-start.3
  1.5 1.8 slice.21
  3.4 0.6 collective-permute-start.5
  3.9 3.6 fusion
  7.5 1.5 collective-permute-start.7
  9.0 0.5 collective-permute-start.1
  9.6 95.1 %collective-permute-done.1 = s32[1024]{0:T(1024)S(1)} collective-permute-done((s32[1024]{0:T(1024)S(1)}, s32[1024]{0:T(1024)S(1)}, u32[]{:S(2)}, u32[]{:S(2)}) %collective-permute-start.1) | collective-permute-done | bytes 4128 | tf_op jit(solution)/shard_map/ppermute | solution.py:300
  104.7 1.2 collective-permute-done
  106.0 1.0 collective-permute-done.2
  107.0 0.5 collective-permute-start.9
  107.5 1.5 collective-permute-start.15
  109.0 50.7 %collective-permute-done.9.refs_4_ = bf16[1280,896]{1,0:T(8,128)(2,1)S(1)} collective-permute-done((bf16[1280,896]{1,0:T(8,128)(2,1)S(1)}, bf16[1280,896]{1,0:T(8,128)(2,1)S(1)}, u32[]{:S(2)}, u32[]{:S(2)}) %collective-permute-start.9) | collective-permute-done | bytes 2293792 | tf_op jit(solution)/shard_map/ppermute | solution.py:300
  159.7 1.5 copy-done.6
  161.2 1.0 copy.7.q_doc
  162.2 46.0 %collective-permute-done.15.refs_4_ = bf16[1280,896]{1,0:T(8,128)(2,1)} collective-permute-done((bf16[1280,896]{1,0:T(8,128)(2,1)S(1)}, bf16[1280,896]{1,0:T(8,128)(2,1)}, u32[]{:S(2)}, u32[]{:S(2)}) %collective-permute-start.15) | collective-permute-done | bytes 2293792 | tf_op jit(solution)/shard_map/ppermute | solution.py:300
  208.2 0.6 pad_add_fusion.k_doc
  208.8 0.5 collective-permute-start.30
  209.3 18.4 %shard_map.46 = (bf16[1024,640]{1,0:T(8,128)(2,1)}, bf16[1024,256]{1,0:T(8,128)(2,1)}) custom-call(bf16[1024,2560]{1,0:T(8,128)(2,1)} %refs_0_.7, bf16[1024,2560]{1,0:T(8,128)(2,1)} %collective-permute-done.3.refs_1_, bf16[1280,3584]{1,0:T(8,128)(2,1)} %refs_2_.7, bf16[1280,3584]{1,0:T(8,128)(2,1)} %collective-permute-done.4.refs_3_, ...), custom_call_target="tpu_custom_call" | custom-call | flops 9395240960 | bytes 19660800 | tf_op jit(solution)/shard_map/pallas_call | solution.py:81
  227.8 1.1 collective-permute-start.11
  228.9 18.4 %shard_map.47 = (bf16[1024,640]{1,0:T(8,128)(2,1)}, bf16[1024,256]{1,0:T(8,128)(2,1)}) custom-call(bf16[1024,2560]{1,0:T(8,128)(2,1)} %refs_0_.7, bf16[1024,2560]{1,0:T(8,128)(2,1)} %collective-permute-done.3.refs_1_, bf16[1280,3584]{1,0:T(8,128)(2,1)} %refs_2_.7, bf16[1280,3584]{1,0:T(8,128)(2,1)} %collective-permute-done.4.refs_3_, ...), custom_call_target="tpu_custom_call" | custom-call | flops 9395240960 | bytes 19660800 | tf_op jit(solution)/shard_map/pallas_call | solution.py:81
  247.3 2.5 slice.27
  249.8 3.8 slice.26
  253.6 3.1 slice.25
  257.0 0.6 collective-permute-start.13
  257.6 18.6 %shard_map.48 = (bf16[1024,640]{1,0:T(8,128)(2,1)}, bf16[1024,256]{1,0:T(8,128)(2,1)}) custom-call(bf16[1024,2560]{1,0:T(8,128)(2,1)} %refs_0_.7, bf16[1024,2560]{1,0:T(8,128)(2,1)} %collective-permute-done.3.refs_1_, bf16[1280,3584]{1,0:T(8,128)(2,1)} %refs_2_.7, bf16[1280,3584]{1,0:T(8,128)(2,1)} %collective-permute-done.4.refs_3_, ...), custom_call_target="tpu_custom_call" | custom-call | flops 9395240960 | bytes 19660800 | tf_op jit(solution)/shard_map/pallas_call | solution.py:81
  276.2 0.6 collective-permute-start.17
  277.0 40.1 %shard_map.49.refs_0_ = bf16[1024,640]{1,0:T(8,128)(2,1)} custom-call(s32[4096]{0:T(1024)} %copy-done.5, bf16[1024,640]{1,0:T(8,128)(2,1)} %get-tuple-element.30.q_ref, bf16[1024,256]{1,0:T(8,128)(2,1)} %get-tuple-element.24.k0, bf16[1024,256]{1,0:T(8,128)(2,1)} %collective-permute-done.11.k1, bf16[1024,256]{1,0:T(8,128)(2,1)} %copy-done.13, ...), custom_call_target="tpu_custom_call" | custom-call | flops 42949672960 | bytes 2621440 | tf_op jit(solution)/shard_map/pallas_call | solution.py:284
  317.6 0.9 copy-done.7
  318.5 18.3 %shard_map.50 = (bf16[1024,640]{1,0:T(8,128)(2,1)}, bf16[1024,256]{1,0:T(8,128)(2,1)}) custom-call(bf16[1024,2560]{1,0:T(8,128)(2,1)} %refs_0_.7, bf16[1024,2560]{1,0:T(8,128)(2,1)} %collective-permute-done.3.refs_1_, bf16[1280,3584]{1,0:T(8,128)(2,1)} %refs_2_.7, bf16[1280,3584]{1,0:T(8,128)(2,1)} %collective-permute-done.4.refs_3_, ...), custom_call_target="tpu_custom_call" | custom-call | flops 9395240960 | bytes 19660800 | tf_op jit(solution)/shard_map/pallas_call | solution.py:81
  336.8 4.1 collective-permute-start.35
  341.0 40.0 %shard_map.51.refs_2_ = bf16[1024,640]{1,0:T(8,128)(2,1)} custom-call(s32[4096]{0:T(1024)} %copy-done.5, bf16[1024,640]{1,0:T(8,128)(2,1)} %get-tuple-element.34.q_ref, bf16[1024,256]{1,0:T(8,128)(2,1)} %get-tuple-element.27.k0, bf16[1024,256]{1,0:T(8,128)(2,1)} %collective-permute-done.17.k1, bf16[1024,256]{1,0:T(8,128)(2,1)} %copy-done.12, ...), custom_call_target="tpu_custom_call" | custom-call | flops 42949672960 | bytes 2621440 | tf_op jit(solution)/shard_map/pallas_call | solution.py:284
  381.0 5.5 collective-permute-start.33
  387.3 39.9 %shard_map.52.refs_4_ = bf16[1024,640]{1,0:T(8,128)(2,1)} custom-call(s32[4096]{0:T(1024)} %copy-done.5, bf16[1024,640]{1,0:T(8,128)(2,1)} %get-tuple-element.35.q_ref, bf16[1024,256]{1,0:T(8,128)(2,1)} %get-tuple-element.36.k0, bf16[1024,256]{1,0:T(8,128)(2,1)} %collective-permute-done.21.k1, bf16[1024,256]{1,0:T(8,128)(2,1)} %collective-permute-done.22.k2, ...), custom_call_target="tpu_custom_call" | custom-call | flops 42949672960 | bytes 2621440 | tf_op jit(solution)/shard_map/pallas_call | solution.py:284
  427.2 3.7 collective-permute-start.31
  431.4 27.1 %collective-permute-done.33.refs_12_ = bf16[1280,1280]{1,0:T(8,128)(2,1)} collective-permute-done((bf16[1280,1280]{1,0:T(8,128)(2,1)}, bf16[1280,1280]{1,0:T(8,128)(2,1)}, u32[]{:S(2)}, u32[]{:S(2)}) %collective-permute-start.33) | collective-permute-done | bytes 3276832 | tf_op jit(solution)/shard_map/ppermute | solution.py:300
  458.6 22.5 %shard_map.53.refs_6_ = bf16[512,640]{1,0:T(8,128)(2,1)} custom-call(s32[4096]{0:T(1024)} %copy-done.5, bf16[1024,640]{1,0:T(8,128)(2,1)} %get-tuple-element.39.q_ref, bf16[1024,256]{1,0:T(8,128)(2,1)} %get-tuple-element.38.k0, bf16[1024,256]{1,0:T(8,128)(2,1)} %collective-permute-done.25.k1, bf16[1024,256]{1,0:T(8,128)(2,1)} %copy-done.11, ...), custom_call_target="tpu_custom_call" | custom-call | flops 21474836480 | bytes 1310720 | tf_op jit(solution)/shard_map/pallas_call | solution.py:284
  481.1 0.5 collective-permute-start.20
  481.6 1.6 collective-permute-start.14
  483.2 13.5 %collective-permute-done.31.refs_12_ = bf16[1280,768]{1,0:T(8,128)(2,1)} collective-permute-done((bf16[1280,768]{1,0:T(8,128)(2,1)}, bf16[1280,768]{1,0:T(8,128)(2,1)}, u32[]{:S(2)}, u32[]{:S(2)}) %collective-permute-start.31) | collective-permute-done | bytes 1966112 | tf_op jit(solution)/shard_map/ppermute | solution.py:300
  496.7 22.6 %shard_map.54.refs_8_ = bf16[512,640]{1,0:T(8,128)(2,1)} custom-call(s32[4096]{0:T(1024)} %copy-done.5, bf16[1024,640]{1,0:T(8,128)(2,1)} %get-tuple-element.39.q_ref, bf16[1024,256]{1,0:T(8,128)(2,1)} %get-tuple-element.38.k0, bf16[1024,256]{1,0:T(8,128)(2,1)} %collective-permute-done.25.k1, bf16[1024,256]{1,0:T(8,128)(2,1)} %copy-done.11, ...), custom_call_target="tpu_custom_call" | custom-call | flops 21474836480 | bytes 1310720 | tf_op jit(solution)/shard_map/pallas_call | solution.py:284
  519.8 1.6 collective-permute-start.28
  521.3 19.6 %collective-permute-done.14.refs_1_ = bf16[1024,640]{1,0:T(8,128)(2,1)} collective-permute-done((bf16[1024,640]{1,0:T(8,128)(2,1)S(1)}, bf16[1024,640]{1,0:T(8,128)(2,1)}, u32[]{:S(2)}, u32[]{:S(2)}) %collective-permute-start.14) | collective-permute-done | bytes 1310752 | tf_op jit(solution)/shard_map/ppermute | solution.py:337
  541.0 14.0 %collective-permute-done.29.refs_9_ = bf16[512,640]{1,0:T(8,128)(2,1)} collective-permute-done((bf16[512,640]{1,0:T(8,128)(2,1)}, bf16[512,640]{1,0:T(8,128)(2,1)}, u32[]{:S(2)}, u32[]{:S(2)}) %collective-permute-start.29) | collective-permute-done | bytes 655392 | tf_op jit(solution)/shard_map/ppermute | solution.py:337
  555.0 13.5 %collective-permute-done.28.refs_7_ = bf16[512,640]{1,0:T(8,128)(2,1)S(1)} collective-permute-done((bf16[512,640]{1,0:T(8,128)(2,1)}, bf16[512,640]{1,0:T(8,128)(2,1)S(1)}, u32[]{:S(2)}, u32[]{:S(2)}) %collective-permute-start.28) | collective-permute-done | bytes 655392 | tf_op jit(solution)/shard_map/ppermute | solution.py:337
  568.5 0.8 copy-done.3
  569.3 12.5 %shard_map.55.refs_14_ = bf16[1024,2560]{1,0:T(8,128)(2,1)} custom-call(bf16[1024,640]{1,0:T(8,128)(2,1)} %shard_map.49.refs_0_, bf16[1024,640]{1,0:T(8,128)(2,1)} %collective-permute-done.14.refs_1_, bf16[1024,640]{1,0:T(8,128)(2,1)} %shard_map.51.refs_2_, bf16[1024,640]{1,0:T(8,128)(2,1)} %collective-permute-done.20.refs_3_, ...), custom_call_target="tpu_custom_call" | custom-call | flops 5368709120 | bytes 15728640 | tf_op jit(solution)/shard_map/pallas_call | solution.py:136
  581.9 21.4 %shard_map.56.refs_14_ = bf16[1024,2560]{1,0:T(8,128)(2,1)} custom-call(bf16[1024,640]{1,0:T(8,128)(2,1)} %shard_map.49.refs_0_, bf16[1024,640]{1,0:T(8,128)(2,1)} %collective-permute-done.14.refs_1_, bf16[1024,640]{1,0:T(8,128)(2,1)} %shard_map.51.refs_2_, bf16[1024,640]{1,0:T(8,128)(2,1)} %collective-permute-done.20.refs_3_, ...), custom_call_target="tpu_custom_call", output_to_operand_aliasing={{}: (14, {})} | custom-call | flops 13421772800 | bytes 23592960 | tf_op jit(solution)/shard_map/pallas_call | solution.py:136
  603.2 15.5 %shard_map.57 = bf16[1024,2560]{1,0:T(8,128)(2,1)} custom-call(bf16[1024,640]{1,0:T(8,128)(2,1)} %shard_map.49.refs_0_, bf16[1024,640]{1,0:T(8,128)(2,1)} %collective-permute-done.14.refs_1_, bf16[1024,640]{1,0:T(8,128)(2,1)} %shard_map.51.refs_2_, bf16[1024,640]{1,0:T(8,128)(2,1)} %collective-permute-done.20.refs_3_, ...), custom_call_target="tpu_custom_call", output_to_operand_aliasing={{}: (14, {})} | custom-call | flops 8053063680 | bytes 18350080 | tf_op jit(solution)/shard_map/pallas_call | solution.py:136
  (79 shorter events, 3.0 us)
Async XLA Ops:
  0.0 209.3 %collective-permute-start.4 = (bf16[1280,3584]{1,0:T(8,128)(2,1)}, bf16[1280,3584]{1,0:T(8,128)(2,1)}, u32[]{:S(2)}, u32[]{:S(2)}) collective-permute-start(bf16[1280,3584]{1,0:T(8,128)(2,1)} %refs_2_.7), channel_id=1, source_target_pairs={{0,1},{1,0},{2,3},{3,2},{4,5},{5,4},{6,7},{7,6}} | collective-permute-start | bytes 27525128 | tf_op jit(solution)/shard_map/ppermute | solution.py:303
  0.0 209.3 %collective-permute-start.3 = (bf16[1024,2560]{1,0:T(8,128)(2,1)}, bf16[1024,2560]{1,0:T(8,128)(2,1)}, u32[]{:S(2)}, u32[]{:S(2)}) collective-permute-start(bf16[1024,2560]{1,0:T(8,128)(2,1)} %refs_0_.7), channel_id=1, source_target_pairs={{0,4},{4,0},{1,5},{5,1},{2,6},{6,2},{3,7},{7,3}} | collective-permute-start | bytes 15728648 | tf_op jit(solution)/shard_map/ppermute | solution.py:316
  3.4 5.7 copy-start.4
  3.4 104.2 %collective-permute-start.5 = (bf16[1280,896]{1,0:T(8,128)(2,1)S(1)}, bf16[1280,896]{1,0:T(8,128)(2,1)}, u32[]{:S(2)}, u32[]{:S(2)}) collective-permute-start(bf16[1280,896]{1,0:T(8,128)(2,1)S(1)} %slice.21), channel_id=1, source_target_pairs={{0,2},{1,3},{2,0},{3,1},{4,6},{5,7},{6,4},{7,5}} | collective-permute-start | bytes 6881288 | tf_op jit(solution)/shard_map/ppermute | solution.py:300
  7.5 101.5 %collective-permute-start.7 = (bf16[1280,896]{1,0:T(8,128)(2,1)S(1)}, bf16[1280,896]{1,0:T(8,128)(2,1)}, u32[]{:S(2)}, u32[]{:S(2)}) collective-permute-start(bf16[1280,896]{1,0:T(8,128)(2,1)S(1)} %get-tuple-element.43), channel_id=1, source_target_pairs={{0,2},{1,3},{2,0},{3,1},{4,6},{5,7},{6,4},{7,5}} | collective-permute-start | bytes 6881288 | tf_op jit(solution)/shard_map/ppermute | solution.py:300
  9.0 95.6 %collective-permute-start.1 = (s32[1024]{0:T(1024)S(1)}, s32[1024]{0:T(1024)S(1)}, u32[]{:S(2)}, u32[]{:S(2)}) collective-permute-start(s32[1024]{0:T(1024)S(1)} %copy-done.4), channel_id=1, source_target_pairs={{0,2},{1,3},{2,0},{3,1},{4,6},{5,7},{6,4},{7,5}} | collective-permute-start | bytes 12296 | tf_op jit(solution)/shard_map/ppermute | solution.py:300
  104.7 1.2 collective-permute-start
  105.8 1.2 collective-permute-start.2
  107.0 52.7 %collective-permute-start.9 = (bf16[1280,896]{1,0:T(8,128)(2,1)S(1)}, bf16[1280,896]{1,0:T(8,128)(2,1)S(1)}, u32[]{:S(2)}, u32[]{:S(2)}) collective-permute-start(bf16[1280,896]{1,0:T(8,128)(2,1)S(1)} %get-tuple-element.42), channel_id=1, source_target_pairs={{0,2},{1,3},{2,0},{3,1},{4,6},{5,7},{6,4},{7,5}} | collective-permute-start | bytes 6881288 | tf_op jit(solution)/shard_map/ppermute | solution.py:300
  107.5 100.6 %collective-permute-start.15 = (bf16[1280,896]{1,0:T(8,128)(2,1)S(1)}, bf16[1280,896]{1,0:T(8,128)(2,1)}, u32[]{:S(2)}, u32[]{:S(2)}) collective-permute-start(bf16[1280,896]{1,0:T(8,128)(2,1)S(1)} %get-tuple-element.41), channel_id=1, source_target_pairs={{0,2},{1,3},{2,0},{3,1},{4,6},{5,7},{6,4},{7,5}} | collective-permute-start | bytes 6881288 | tf_op jit(solution)/shard_map/ppermute | solution.py:300
  109.0 99.8 %collective-permute-start.6 = (bf16[1280,896]{1,0:T(8,128)(2,1)}, bf16[1280,896]{1,0:T(8,128)(2,1)}, u32[]{:S(2)}, u32[]{:S(2)}) collective-permute-start(bf16[1280,896]{1,0:T(8,128)(2,1)} %collective-permute-done.5.refs_4_), channel_id=1, source_target_pairs={{0,1},{1,0},{2,3},{3,2},{4,5},{5,4},{6,7},{7,6}} | collective-permute-start | bytes 6881288 | tf_op jit(solution)/shard_map/ppermute | solution.py:303
  161.2 66.7 %collective-permute-start.8 = (bf16[1280,896]{1,0:T(8,128)(2,1)}, bf16[1280,896]{1,0:T(8,128)(2,1)}, u32[]{:S(2)}, u32[]{:S(2)}) collective-permute-start(bf16[1280,896]{1,0:T(8,128)(2,1)} %collective-permute-done.7.refs_4_), channel_id=1, source_target_pairs={{0,1},{1,0},{2,3},{3,2},{4,5},{5,4},{6,7},{7,6}} | collective-permute-start | bytes 6881288 | tf_op jit(solution)/shard_map/ppermute | solution.py:303
  208.2 48.6 %collective-permute-start.10 = (bf16[1280,896]{1,0:T(8,128)(2,1)}, bf16[1280,896]{1,0:T(8,128)(2,1)}, u32[]{:S(2)}, u32[]{:S(2)}) collective-permute-start(bf16[1280,896]{1,0:T(8,128)(2,1)} %copy-done.6), channel_id=1, source_target_pairs={{0,1},{1,0},{2,3},{3,2},{4,5},{5,4},{6,7},{7,6}} | collective-permute-start | bytes 6881288 | tf_op jit(solution)/shard_map/ppermute | solution.py:303
  208.2 19.6 %copy-start.5 = (s32[4096]{0:T(1024)}, s32[4096]{0:T(1024)S(1)}, u32[]{:S(2)}) copy-start(s32[4096]{0:T(1024)S(1)} %constant_dynamic-update-slice_fusion.docs) | copy-start | bytes 49156
  208.8 272.3 %collective-permute-start.30 = (bf16[1280,2560]{1,0:T(8,128)(2,1)}, bf16[1280,2560]{1,0:T(8,128)(2,1)}, u32[]{:S(2)}, u32[]{:S(2)}) collective-permute-start(bf16[1280,2560]{1,0:T(8,128)(2,1)} %refs_10_.5), channel_id=1, source_target_pairs={{0,1},{1,0},{2,3},{3,2},{4,5},{5,4},{6,7},{7,6}} | collective-permute-start | bytes 19660808 | tf_op jit(solution)/shard_map/ppermute | solution.py:303
  209.3 107.7 %collective-permute-start.16 = (bf16[1280,896]{1,0:T(8,128)(2,1)}, bf16[1280,896]{1,0:T(8,128)(2,1)S(1)}, u32[]{:S(2)}, u32[]{:S(2)}) collective-permute-start(bf16[1280,896]{1,0:T(8,128)(2,1)} %collective-permute-done.15.refs_4_), channel_id=1, source_target_pairs={{0,1},{1,0},{2,3},{3,2},{4,5},{5,4},{6,7},{7,6}} | collective-permute-start | bytes 6881288 | tf_op jit(solution)/shard_map/ppermute | solution.py:303
  227.8 29.2 %collective-permute-start.12 = (bf16[1024,256]{1,0:T(8,128)(2,1)}, bf16[1024,256]{1,0:T(8,128)(2,1)S(1)}, u32[]{:S(2)}, u32[]{:S(2)}) collective-permute-start(bf16[1024,256]{1,0:T(8,128)(2,1)} %get-tuple-element.24.k0), channel_id=1, source_target_pairs={{0,2},{1,3},{2,0},{3,1},{4,6},{5,7},{6,4},{7,5}} | collective-permute-start | bytes 1572872 | tf_op jit(solution)/shard_map/ppermute | solution.py:300
  227.8 48.3 %collective-permute-start.11 = (bf16[1024,256]{1,0:T(8,128)(2,1)}, bf16[1024,256]{1,0:T(8,128)(2,1)}, u32[]{:S(2)}, u32[]{:S(2)}) collective-permute-start(bf16[1024,256]{1,0:T(8,128)(2,1)} %get-tuple-element.24.k0), channel_id=1, source_target_pairs={{0,1},{1,0},{2,3},{3,2},{4,5},{5,4},{6,7},{7,6}} | collective-permute-start | bytes 1572872 | tf_op jit(solution)/shard_map/ppermute | solution.py:303
  253.6 3.1 copy-start.10
  256.8 60.4 %collective-permute-start.18 = (bf16[1024,256]{1,0:T(8,128)(2,1)S(1)}, bf16[1024,256]{1,0:T(8,128)(2,1)S(1)}, u32[]{:S(2)}, u32[]{:S(2)}) collective-permute-start(bf16[1024,256]{1,0:T(8,128)(2,1)S(1)} %copy-done.10), channel_id=1, source_target_pairs={{0,2},{1,3},{2,0},{3,1},{4,6},{5,7},{6,4},{7,5}} | collective-permute-start | bytes 1572872 | tf_op jit(solution)/shard_map/ppermute | solution.py:300
  257.0 19.2 %copy-start.13 = (bf16[1024,256]{1,0:T(8,128)(2,1)}, bf16[1024,256]{1,0:T(8,128)(2,1)S(1)}, u32[]{:S(2)}) copy-start(bf16[1024,256]{1,0:T(8,128)(2,1)S(1)} %collective-permute-done.12.k2) | copy-start | bytes 1572868
  257.0 19.8 %collective-permute-start.13 = (bf16[1024,256]{1,0:T(8,128)(2,1)S(1)}, bf16[1024,256]{1,0:T(8,128)(2,1)}, u32[]{:S(2)}, u32[]{:S(2)}) collective-permute-start(bf16[1024,256]{1,0:T(8,128)(2,1)S(1)} %collective-permute-done.12.k2), channel_id=1, source_target_pairs={{0,1},{1,0},{2,3},{3,2},{4,5},{5,4},{6,7},{7,6}} | collective-permute-start | bytes 1572872 | tf_op jit(solution)/shard_map/ppermute | solution.py:303
  276.2 60.6 %collective-permute-start.17 = (bf16[1024,256]{1,0:T(8,128)(2,1)S(1)}, bf16[1024,256]{1,0:T(8,128)(2,1)}, u32[]{:S(2)}, u32[]{:S(2)}) collective-permute-start(bf16[1024,256]{1,0:T(8,128)(2,1)S(1)} %copy-done.10), channel_id=1, source_target_pairs={{0,1},{1,0},{2,3},{3,2},{4,5},{5,4},{6,7},{7,6}} | collective-permute-start | bytes 1572872 | tf_op jit(solution)/shard_map/ppermute | solution.py:303
  276.8 40.3 %copy-start.9 = (bf16[1024,256]{1,0:T(8,128)(2,1)S(1)}, bf16[1024,256]{1,0:T(8,128)(2,1)}, u32[]{:S(2)}) copy-start(bf16[1024,256]{1,0:T(8,128)(2,1)} %get-tuple-element.36.k0) | copy-start | bytes 1572868
  276.8 64.1 %collective-permute-start.22 = (bf16[1024,256]{1,0:T(8,128)(2,1)}, bf16[1024,256]{1,0:T(8,128)(2,1)}, u32[]{:S(2)}, u32[]{:S(2)}) collective-permute-start(bf16[1024,256]{1,0:T(8,128)(2,1)} %get-tuple-element.36.k0), channel_id=1, source_target_pairs={{0,2},{1,3},{2,0},{3,1},{4,6},{5,7},{6,4},{7,5}} | collective-permute-start | bytes 1572872 | tf_op jit(solution)/shard_map/ppermute | solution.py:300
  317.1 63.9 %collective-permute-start.21 = (bf16[1024,256]{1,0:T(8,128)(2,1)S(1)}, bf16[1024,256]{1,0:T(8,128)(2,1)}, u32[]{:S(2)}, u32[]{:S(2)}) collective-permute-start(bf16[1024,256]{1,0:T(8,128)(2,1)S(1)} %copy-done.9), channel_id=1, source_target_pairs={{0,1},{1,0},{2,3},{3,2},{4,5},{5,4},{6,7},{7,6}} | collective-permute-start | bytes 1572872 | tf_op jit(solution)/shard_map/ppermute | solution.py:303
  317.2 19.6 %copy-start.12 = (bf16[1024,256]{1,0:T(8,128)(2,1)}, bf16[1024,256]{1,0:T(8,128)(2,1)S(1)}, u32[]{:S(2)}) copy-start(bf16[1024,256]{1,0:T(8,128)(2,1)S(1)} %collective-permute-done.18.k2) | copy-start | bytes 1572868
  317.2 23.7 %collective-permute-start.19 = (bf16[1024,256]{1,0:T(8,128)(2,1)S(1)}, bf16[1024,256]{1,0:T(8,128)(2,1)}, u32[]{:S(2)}, u32[]{:S(2)}) collective-permute-start(bf16[1024,256]{1,0:T(8,128)(2,1)S(1)} %collective-permute-done.18.k2), channel_id=1, source_target_pairs={{0,1},{1,0},{2,3},{3,2},{4,5},{5,4},{6,7},{7,6}} | collective-permute-start | bytes 1572872 | tf_op jit(solution)/shard_map/ppermute | solution.py:303
  336.8 144.8 %collective-permute-start.35 = (bf16[1280,512]{1,0:T(8,128)(2,1)}, bf16[1280,512]{1,0:T(8,128)(2,1)}, u32[]{:S(2)}, u32[]{:S(2)}) collective-permute-start(bf16[1280,512]{1,0:T(8,128)(2,1)} %slice.27), channel_id=1, source_target_pairs={{0,2},{1,3},{2,0},{3,1},{4,6},{5,7},{6,4},{7,5}} | collective-permute-start | bytes 3932168 | tf_op jit(solution)/shard_map/ppermute | solution.py:300
  340.9 45.6 %collective-permute-start.23 = (bf16[1024,256]{1,0:T(8,128)(2,1)}, bf16[1024,256]{1,0:T(8,128)(2,1)S(1)}, u32[]{:S(2)}, u32[]{:S(2)}) collective-permute-start(bf16[1024,256]{1,0:T(8,128)(2,1)} %collective-permute-done.22.k2), channel_id=1, source_target_pairs={{0,1},{1,0},{2,3},{3,2},{4,5},{5,4},{6,7},{7,6}} | collective-permute-start | bytes 1572872 | tf_op jit(solution)/shard_map/ppermute | solution.py:303
  340.9 45.6 %copy-start.8 = (bf16[1024,256]{1,0:T(8,128)(2,1)S(1)}, bf16[1024,256]{1,0:T(8,128)(2,1)}, u32[]{:S(2)}) copy-start(bf16[1024,256]{1,0:T(8,128)(2,1)} %get-tuple-element.38.k0) | copy-start | bytes 1572868
  340.9 45.6 %collective-permute-start.26 = (bf16[1024,256]{1,0:T(8,128)(2,1)}, bf16[1024,256]{1,0:T(8,128)(2,1)S(1)}, u32[]{:S(2)}, u32[]{:S(2)}) collective-permute-start(bf16[1024,256]{1,0:T(8,128)(2,1)} %get-tuple-element.38.k0), channel_id=1, source_target_pairs={{0,2},{1,3},{2,0},{3,1},{4,6},{5,7},{6,4},{7,5}} | collective-permute-start | bytes 1572872 | tf_op jit(solution)/shard_map/ppermute | solution.py:300
  381.0 77.6 %collective-permute-start.33 = (bf16[1280,1280]{1,0:T(8,128)(2,1)}, bf16[1280,1280]{1,0:T(8,128)(2,1)}, u32[]{:S(2)}, u32[]{:S(2)}) collective-permute-start(bf16[1280,1280]{1,0:T(8,128)(2,1)} %slice.26), channel_id=1, source_target_pairs={{0,2},{1,3},{2,0},{3,1},{4,6},{5,7},{6,4},{7,5}} | collective-permute-start | bytes 9830408 | tf_op jit(solution)/shard_map/ppermute | solution.py:300
  386.5 40.7 %collective-permute-start.25 = (bf16[1024,256]{1,0:T(8,128)(2,1)S(1)}, bf16[1024,256]{1,0:T(8,128)(2,1)}, u32[]{:S(2)}, u32[]{:S(2)}) collective-permute-start(bf16[1024,256]{1,0:T(8,128)(2,1)S(1)} %copy-done.8), channel_id=1, source_target_pairs={{0,1},{1,0},{2,3},{3,2},{4,5},{5,4},{6,7},{7,6}} | collective-permute-start | bytes 1572872 | tf_op jit(solution)/shard_map/ppermute | solution.py:303
  386.5 40.6 %copy-start.11 = (bf16[1024,256]{1,0:T(8,128)(2,1)}, bf16[1024,256]{1,0:T(8,128)(2,1)S(1)}, u32[]{:S(2)}) copy-start(bf16[1024,256]{1,0:T(8,128)(2,1)S(1)} %collective-permute-done.26.k2) | copy-start | bytes 1572868
  386.6 44.4 %collective-permute-start.27 = (bf16[1024,256]{1,0:T(8,128)(2,1)S(1)}, bf16[1024,256]{1,0:T(8,128)(2,1)}, u32[]{:S(2)}, u32[]{:S(2)}) collective-permute-start(bf16[1024,256]{1,0:T(8,128)(2,1)S(1)} %collective-permute-done.26.k2), channel_id=1, source_target_pairs={{0,1},{1,0},{2,3},{3,2},{4,5},{5,4},{6,7},{7,6}} | collective-permute-start | bytes 1572872 | tf_op jit(solution)/shard_map/ppermute | solution.py:303
  427.2 53.9 %copy-start.1 = (bf16[1024,640]{1,0:T(8,128)(2,1)S(1)}, bf16[1024,640]{1,0:T(8,128)(2,1)}, u32[]{:S(2)}) copy-start(bf16[1024,640]{1,0:T(8,128)(2,1)} %shard_map.51.refs_2_) | copy-start | bytes 3932164
  427.2 54.4 %copy-start = (bf16[1024,640]{1,0:T(8,128)(2,1)S(1)}, bf16[1024,640]{1,0:T(8,128)(2,1)}, u32[]{:S(2)}) copy-start(bf16[1024,640]{1,0:T(8,128)(2,1)} %shard_map.49.refs_0_) | copy-start | bytes 3932164
  427.2 69.4 %collective-permute-start.31 = (bf16[1280,768]{1,0:T(8,128)(2,1)}, bf16[1280,768]{1,0:T(8,128)(2,1)}, u32[]{:S(2)}, u32[]{:S(2)}) collective-permute-start(bf16[1280,768]{1,0:T(8,128)(2,1)} %slice.25), channel_id=1, source_target_pairs={{0,2},{1,3},{2,0},{3,1},{4,6},{5,7},{6,4},{7,5}} | collective-permute-start | bytes 5898248 | tf_op jit(solution)/shard_map/ppermute | solution.py:300
  431.0 88.3 %collective-permute-start.24 = (bf16[1024,640]{1,0:T(8,128)(2,1)}, bf16[1024,640]{1,0:T(8,128)(2,1)S(1)}, u32[]{:S(2)}, u32[]{:S(2)}) collective-permute-start(bf16[1024,640]{1,0:T(8,128)(2,1)} %shard_map.52.refs_4_), channel_id=1, source_target_pairs={{0,4},{4,0},{1,5},{5,1},{2,6},{6,2},{3,7},{7,3}} | collective-permute-start | bytes 3932168 | tf_op jit(solution)/shard_map/ppermute | solution.py:337
  458.6 123.3 %collective-permute-start.34 = (bf16[1280,1280]{1,0:T(8,128)(2,1)}, bf16[1280,1280]{1,0:T(8,128)(2,1)}, u32[]{:S(2)}, u32[]{:S(2)}) collective-permute-start(bf16[1280,1280]{1,0:T(8,128)(2,1)} %collective-permute-done.33.refs_12_), channel_id=1, source_target_pairs={{0,1},{1,0},{2,3},{3,2},{4,5},{5,4},{6,7},{7,6}} | collective-permute-start | bytes 9830408 | tf_op jit(solution)/shard_map/ppermute | solution.py:303
  481.1 38.7 %collective-permute-start.20 = (bf16[1024,640]{1,0:T(8,128)(2,1)S(1)}, bf16[1024,640]{1,0:T(8,128)(2,1)}, u32[]{:S(2)}, u32[]{:S(2)}) collective-permute-start(bf16[1024,640]{1,0:T(8,128)(2,1)S(1)} %copy-done.1), channel_id=1, source_target_pairs={{0,4},{4,0},{1,5},{5,1},{2,6},{6,2},{3,7},{7,3}} | collective-permute-start | bytes 3932168 | tf_op jit(solution)/shard_map/ppermute | solution.py:337
  481.6 59.4 %collective-permute-start.14 = (bf16[1024,640]{1,0:T(8,128)(2,1)S(1)}, bf16[1024,640]{1,0:T(8,128)(2,1)}, u32[]{:S(2)}, u32[]{:S(2)}) collective-permute-start(bf16[1024,640]{1,0:T(8,128)(2,1)S(1)} %copy-done), channel_id=1, source_target_pairs={{0,4},{4,0},{1,5},{5,1},{2,6},{6,2},{3,7},{7,3}} | collective-permute-start | bytes 3932168 | tf_op jit(solution)/shard_map/ppermute | solution.py:337
  496.7 44.3 %collective-permute-start.36 = (bf16[1280,512]{1,0:T(8,128)(2,1)}, bf16[1280,512]{1,0:T(8,128)(2,1)}, u32[]{:S(2)}, u32[]{:S(2)}) collective-permute-start(bf16[1280,512]{1,0:T(8,128)(2,1)} %collective-permute-done.35.refs_12_), channel_id=1, source_target_pairs={{0,1},{1,0},{2,3},{3,2},{4,5},{5,4},{6,7},{7,6}} | collective-permute-start | bytes 3932168 | tf_op jit(solution)/shard_map/ppermute | solution.py:303
  519.3 49.2 %copy-start.2 = (bf16[1024,640]{1,0:T(8,128)(2,1)}, bf16[1024,640]{1,0:T(8,128)(2,1)S(1)}, u32[]{:S(2)}) copy-start(bf16[1024,640]{1,0:T(8,128)(2,1)S(1)} %collective-permute-done.24.refs_5_) | copy-start | bytes 3932164
  519.3 35.7 %collective-permute-start.29 = (bf16[512,640]{1,0:T(8,128)(2,1)}, bf16[512,640]{1,0:T(8,128)(2,1)}, u32[]{:S(2)}, u32[]{:S(2)}) collective-permute-start(bf16[512,640]{1,0:T(8,128)(2,1)} %shard_map.54.refs_8_), channel_id=1, source_target_pairs={{0,4},{4,0},{1,5},{5,1},{2,6},{6,2},{3,7},{7,3}} | collective-permute-start | bytes 1966088 | tf_op jit(solution)/shard_map/ppermute | solution.py:337
  519.8 48.7 %collective-permute-start.28 = (bf16[512,640]{1,0:T(8,128)(2,1)}, bf16[512,640]{1,0:T(8,128)(2,1)S(1)}, u32[]{:S(2)}, u32[]{:S(2)}) collective-permute-start(bf16[512,640]{1,0:T(8,128)(2,1)} %shard_map.53.refs_6_), channel_id=1, source_target_pairs={{0,4},{4,0},{1,5},{5,1},{2,6},{6,2},{3,7},{7,3}} | collective-permute-start | bytes 1966088 | tf_op jit(solution)/shard_map/ppermute | solution.py:337
  541.0 62.3 %collective-permute-start.32 = (bf16[1280,768]{1,0:T(8,128)(2,1)}, bf16[1280,768]{1,0:T(8,128)(2,1)}, u32[]{:S(2)}, u32[]{:S(2)}) collective-permute-start(bf16[1280,768]{1,0:T(8,128)(2,1)} %collective-permute-done.31.refs_12_), channel_id=1, source_target_pairs={{0,1},{1,0},{2,3},{3,2},{4,5},{5,4},{6,7},{7,6}} | collective-permute-start | bytes 5898248 | tf_op jit(solution)/shard_map/ppermute | solution.py:303
  (4 other events, 4.6 us)
